TPU v7x, 32 devices: a whole 2x2x4 slice. The times are simulated.
32 devices in a mesh: seq: 4 (over y, x), fsdp: 8 (over z, core).
Axes of the slice: x: 2, y: 2, z: 4, core: 2. Of those that a mesh axis runs over, the one named last changes fastest.
Arguments:
- tokens: bfloat16 [16, 1568, 1024], P('fsdp', 'seq'), may hold values from -6 to 6
- lengths: int32 [16], P('fsdp'), may hold values from 392 to 1568, as said below
- ln1_gain: bfloat16 [1024], P('fsdp'), may hold values from 0.5 to 1.5
- ln1_bias: bfloat16 [1024], P('fsdp'), may hold values from -2 to 2
- w_qkv: bfloat16 [1024, 3072], P('fsdp'), may hold values from -0.1875 to 0.1875
- q_bias: bfloat16 [1024], P('fsdp'), may hold values from -3 to 3
- v_bias: bfloat16 [1024], P('fsdp'), may hold values from -3 to 3
- w_out: bfloat16 [1024, 1024], P('fsdp'), may hold values from -4 to 4
- b_out: bfloat16 [1024], P('fsdp'), may hold values from -2 to 2
- ln2_gain: bfloat16 [1024], P('fsdp'), may hold values from 0.5 to 1.5
- ln2_bias: bfloat16 [1024], P('fsdp'), may hold values from -2 to 2
- w_fc1: bfloat16 [1024, 4096], P('fsdp'), may hold values from -0.1875 to 0.1875
- b_fc1: bfloat16 [4096], P('fsdp'), may hold values from -2 to 2
- w_fc2: bfloat16 [4096, 1024], P('fsdp'), may hold values from -0.09375 to 0.09375
- b_fc2: bfloat16 [1024], P('fsdp'), may hold values from -2 to 2
- cotangent: bfloat16 [16, 1568, 1024], P('fsdp', 'seq'), may hold values from -6 to 6
Outputs:
- layer_out: bfloat16 [16, 1568, 1024], P('fsdp', 'seq')
- grad_tokens: float32 [16, 1568, 1024], P('fsdp', 'seq')
- grad_ln1_gain: float32 [1024], P('fsdp')
- grad_ln1_bias: float32 [1024], P('fsdp')
- grad_w_qkv: float32 [1024, 3072], P('fsdp')
- grad_q_bias: float32 [1024], P('fsdp')
- grad_v_bias: float32 [1024], P('fsdp')
- grad_w_out: float32 [1024, 1024], P('fsdp')
- grad_b_out: float32 [1024], P('fsdp')
- grad_ln2_gain: float32 [1024], P('fsdp')
- grad_ln2_bias: float32 [1024], P('fsdp')
- grad_w_fc1: float32 [1024, 4096], P('fsdp')
- grad_b_fc1: float32 [4096], P('fsdp')
- grad_w_fc2: float32 [4096, 1024], P('fsdp')
- grad_b_fc2: float32 [1024], P('fsdp')
Inputs may be any that keep to these rules, and one draw needn't show every extreme that they name: `lengths`: the valid tokens of a clip are its first ones; some clip is full and some has exactly 392.
All inputs are finite; a program needn't handle non-finite values.
Results may differ from a plain program's by a relative error of at most 0.018.
Values may be sent and summed in bfloat16 or wider, within the bound.
No kernel may reach another device: no remote copies, remote signals or barrier semaphores. Data moves between devices by JAX's collectives and lax.ppermute only.
A program may use at most 192 MiB of HBM per device.

v0:
```python
from functools import partial

import jax
import jax.numpy as jnp
from jax import lax
from jax.sharding import PartitionSpec as P

HEAD_DIM = 64


EPSILON = 1e-06
NEGATIVE = -1e30


def layer_norm(values, gain, shift):
    centered = values - jnp.mean(values, axis=-1, keepdims=True)
    variance = jnp.mean(centered * centered, axis=-1, keepdims=True)
    return centered * lax.rsqrt(variance + EPSILON) * gain + shift


def split_heads(block, head_count):
    return block.reshape(block.shape[0], head_count, HEAD_DIM).transpose(1, 0, 2)


def merge_heads(block):
    head_count, seq_len, width = block.shape
    return block.transpose(1, 0, 2).reshape(seq_len, head_count * width)


def attend_clip(packed):
    queries, keys, values, length = packed
    seq_len, local_width = queries.shape
    head_count = local_width // HEAD_DIM
    scale = HEAD_DIM ** (-0.5)
    valid = lax.iota(jnp.int32, seq_len) < length
    query_heads = split_heads(queries, head_count).reshape(head_count, 2, seq_len // 2, HEAD_DIM)
    key_heads = split_heads(keys, head_count)
    value_heads = split_heads(values, head_count)

    def per_head(head_set):
        query_blocks, head_keys, head_values = head_set

        def per_block(query_rows):
            raw = jnp.einsum("qd,kd->qk", query_rows, head_keys, preferred_element_type=jnp.float32)
            scores = jnp.where(valid[None, :], raw * scale, NEGATIVE)
            peaks = jnp.max(scores, axis=-1, keepdims=True)
            weights = jnp.exp(scores - peaks)
            totals = jnp.sum(weights, axis=-1, keepdims=True)
            probs = (weights / totals).astype(jnp.bfloat16)
            attended = jnp.einsum(
                "qk,kd->qd", probs, head_values, preferred_element_type=jnp.float32
            )
            return (attended.astype(jnp.bfloat16), (peaks + jnp.log(totals))[:, 0])

        return lax.map(per_block, query_blocks)

    attended, log_totals = lax.map(per_head, (query_heads, key_heads, value_heads))
    return (merge_heads(attended.reshape(head_count, seq_len, HEAD_DIM)), log_totals)


def attend_clip_back(packed):
    queries, keys, values, grads, log_totals, length = packed
    seq_len, local_width = queries.shape
    head_count = local_width // HEAD_DIM
    scale = HEAD_DIM ** (-0.5)
    valid = lax.iota(jnp.int32, seq_len) < length
    query_heads = split_heads(queries, head_count).reshape(head_count, 2, seq_len // 2, HEAD_DIM)
    grad_heads = split_heads(grads, head_count).reshape(head_count, 2, seq_len // 2, HEAD_DIM)
    key_heads = split_heads(keys, head_count)
    value_heads = split_heads(values, head_count)

    def per_head(head_set):
        query_blocks, head_keys, head_values, grad_blocks, head_logs = head_set

        def per_block(carry, block_set):
            key_total, value_total = carry
            query_rows, grad_rows, row_logs = block_set
            raw = jnp.einsum("qd,kd->qk", query_rows, head_keys, preferred_element_type=jnp.float32)
            scores = jnp.where(valid[None, :], raw * scale, NEGATIVE)
            probs = jnp.exp(scores - row_logs[:, None])
            value_total = value_total + jnp.einsum(
                "qk,qd->kd",
                probs.astype(jnp.bfloat16),
                grad_rows,
                preferred_element_type=jnp.float32,
            )
            grad_probs = jnp.einsum(
                "qd,kd->qk", grad_rows, head_values, preferred_element_type=jnp.float32
            )
            inner = jnp.sum(probs * grad_probs, axis=-1, keepdims=True)
            grad_raw = (probs * (grad_probs - inner) * scale).astype(jnp.bfloat16)
            grad_query = jnp.einsum(
                "qk,kd->qd", grad_raw, head_keys, preferred_element_type=jnp.float32
            )
            key_total = key_total + jnp.einsum(
                "qk,qd->kd", grad_raw, query_rows, preferred_element_type=jnp.float32
            )
            return ((key_total, value_total), grad_query.astype(jnp.bfloat16))

        empty = jnp.zeros((seq_len, HEAD_DIM), jnp.float32)
        (key_total, value_total), grad_query = lax.scan(
            per_block, (empty, empty), (query_blocks, grad_blocks, head_logs)
        )
        return (
            grad_query.reshape(seq_len, HEAD_DIM),
            key_total.astype(jnp.bfloat16),
            value_total.astype(jnp.bfloat16),
        )

    grad_q, grad_k, grad_v = lax.map(
        per_head, (query_heads, key_heads, value_heads, grad_heads, log_totals)
    )
    return (merge_heads(grad_q), merge_heads(grad_k), merge_heads(grad_v))


def share_mlp(terms):
    owned = (
        lax.psum_scatter(
            terms[0].astype(jnp.bfloat16), "fsdp", scatter_dimension=0, tiled=True
        ).astype(jnp.float32),
        lax.psum_scatter(
            terms[1].astype(jnp.bfloat16), "fsdp", scatter_dimension=0, tiled=True
        ).astype(jnp.float32),
        lax.psum_scatter(
            terms[2].astype(jnp.bfloat16), "fsdp", scatter_dimension=0, tiled=True
        ).astype(jnp.float32),
        lax.psum_scatter(
            terms[3].astype(jnp.bfloat16), "fsdp", scatter_dimension=0, tiled=True
        ).astype(jnp.float32),
        lax.psum_scatter(
            terms[4].astype(jnp.bfloat16), "fsdp", scatter_dimension=0, tiled=True
        ).astype(jnp.float32),
        lax.psum_scatter(
            terms[5].astype(jnp.bfloat16), "fsdp", scatter_dimension=0, tiled=True
        ).astype(jnp.float32),
    )
    return (
        lax.psum(owned[0].astype(jnp.bfloat16), "seq").astype(jnp.float32),
        lax.psum(owned[1].astype(jnp.bfloat16), "seq").astype(jnp.float32),
        lax.psum(owned[2].astype(jnp.bfloat16), "seq").astype(jnp.float32),
        lax.psum(owned[3].astype(jnp.bfloat16), "seq").astype(jnp.float32),
        lax.psum(owned[4].astype(jnp.bfloat16), "seq").astype(jnp.float32),
        lax.psum(owned[5].astype(jnp.bfloat16), "seq").astype(jnp.float32),
    )


def share_attn(terms):
    owned = (
        lax.psum_scatter(
            terms[0].astype(jnp.bfloat16), "fsdp", scatter_dimension=0, tiled=True
        ).astype(jnp.float32),
        lax.psum_scatter(
            terms[1].astype(jnp.bfloat16), "fsdp", scatter_dimension=0, tiled=True
        ).astype(jnp.float32),
        lax.psum_scatter(
            terms[2].astype(jnp.bfloat16), "fsdp", scatter_dimension=0, tiled=True
        ).astype(jnp.float32),
        lax.psum_scatter(
            terms[3].astype(jnp.bfloat16), "fsdp", scatter_dimension=0, tiled=True
        ).astype(jnp.float32),
        lax.psum_scatter(
            terms[4].astype(jnp.bfloat16), "fsdp", scatter_dimension=0, tiled=True
        ).astype(jnp.float32),
        lax.psum_scatter(
            terms[5].astype(jnp.bfloat16), "fsdp", scatter_dimension=0, tiled=True
        ).astype(jnp.float32),
        lax.psum_scatter(
            terms[6].astype(jnp.bfloat16), "fsdp", scatter_dimension=0, tiled=True
        ).astype(jnp.float32),
    )
    return (
        lax.psum(owned[0].astype(jnp.bfloat16), "seq").astype(jnp.float32),
        lax.psum(owned[1].astype(jnp.bfloat16), "seq").astype(jnp.float32),
        lax.psum(owned[2].astype(jnp.bfloat16), "seq").astype(jnp.float32),
        lax.psum(owned[3].astype(jnp.bfloat16), "seq").astype(jnp.float32),
        lax.psum(owned[4].astype(jnp.bfloat16), "seq").astype(jnp.float32),
        lax.psum(owned[5].astype(jnp.bfloat16), "seq").astype(jnp.float32),
        lax.psum(owned[6].astype(jnp.bfloat16), "seq").astype(jnp.float32),
    )


def shards(
    tokens,
    lengths,
    ln1_gain,
    ln1_bias,
    w_qkv,
    q_bias,
    v_bias,
    w_out,
    b_out,
    ln2_gain,
    ln2_bias,
    w_fc1,
    b_fc1,
    w_fc2,
    b_fc2,
    cotangent,
):
    clip_count, row_count, width = tokens.shape
    total_rows = clip_count * row_count
    full_g1, full_b1, full_qkv, full_qb, full_vb, full_wo, full_bo = (
        lax.all_gather(ln1_gain, "fsdp", axis=0, tiled=True),
        lax.all_gather(ln1_bias, "fsdp", axis=0, tiled=True),
        lax.all_gather(w_qkv, "fsdp", axis=0, tiled=True),
        lax.all_gather(q_bias, "fsdp", axis=0, tiled=True),
        lax.all_gather(v_bias, "fsdp", axis=0, tiled=True),
        lax.all_gather(w_out, "fsdp", axis=0, tiled=True),
        lax.all_gather(b_out, "fsdp", axis=0, tiled=True),
    )
    full_g2, full_b2, full_w1, full_c1, full_w2, full_c2 = (
        lax.all_gather(ln2_gain, "fsdp", axis=0, tiled=True),
        lax.all_gather(ln2_bias, "fsdp", axis=0, tiled=True),
        lax.all_gather(w_fc1, "fsdp", axis=0, tiled=True),
        lax.all_gather(b_fc1, "fsdp", axis=0, tiled=True),
        lax.all_gather(w_fc2, "fsdp", axis=0, tiled=True),
        lax.all_gather(b_fc2, "fsdp", axis=0, tiled=True),
    )
    inputs = tokens.astype(jnp.float32).reshape(total_rows, width)
    normed_f, norm1_back = jax.vjp(
        layer_norm, inputs, full_g1.astype(jnp.float32), full_b1.astype(jnp.float32)
    )
    normed = normed_f.astype(jnp.bfloat16)
    projected = jnp.dot(normed, full_qkv, preferred_element_type=jnp.float32)
    queries = (projected[:, :width] + full_qb.astype(jnp.float32)).astype(jnp.bfloat16)
    keys = projected[:, width : 2 * width].astype(jnp.bfloat16)
    values = (projected[:, 2 * width :] + full_vb.astype(jnp.float32)).astype(jnp.bfloat16)
    shape3 = (clip_count, row_count, width)
    query_clips, key_clips, value_clips = (
        lax.all_to_all(queries.reshape(shape3), "seq", split_axis=2, concat_axis=1, tiled=True),
        lax.all_to_all(keys.reshape(shape3), "seq", split_axis=2, concat_axis=1, tiled=True),
        lax.all_to_all(values.reshape(shape3), "seq", split_axis=2, concat_axis=1, tiled=True),
    )
    attended_heads, log_totals = lax.map(
        attend_clip, (query_clips, key_clips, value_clips, lengths)
    )
    attended = lax.all_to_all(
        attended_heads, "seq", split_axis=1, concat_axis=2, tiled=True
    ).reshape(total_rows, width)
    branch = jnp.dot(attended, full_wo, preferred_element_type=jnp.float32) + full_bo.astype(
        jnp.float32
    )
    middle = inputs + branch
    normed2_f, norm2_back = jax.vjp(
        layer_norm, middle, full_g2.astype(jnp.float32), full_b2.astype(jnp.float32)
    )
    normed_two = normed2_f.astype(jnp.bfloat16)
    hidden_pre = jnp.dot(normed_two, full_w1, preferred_element_type=jnp.float32) + full_c1.astype(
        jnp.float32
    )
    hidden_f, gelu_back = jax.vjp(partial(jax.nn.gelu, approximate=False), hidden_pre)
    hidden = hidden_f.astype(jnp.bfloat16)
    mlp_out = jnp.dot(hidden, full_w2, preferred_element_type=jnp.float32) + full_c2.astype(
        jnp.float32
    )
    layer_out = (middle + mlp_out).astype(jnp.bfloat16).reshape(shape3)
    grad_out = cotangent.reshape(total_rows, width)
    grad_out_f = grad_out.astype(jnp.float32)
    grad_w2 = jnp.einsum("tf,td->fd", hidden, grad_out, preferred_element_type=jnp.float32)
    grad_c2 = jnp.sum(grad_out_f, axis=0)
    grad_hidden = jnp.einsum("td,fd->tf", grad_out, full_w2, preferred_element_type=jnp.float32)
    grad_pre = gelu_back(grad_hidden)[0].astype(jnp.bfloat16)
    grad_w1 = jnp.einsum("td,tf->df", normed_two, grad_pre, preferred_element_type=jnp.float32)
    grad_c1 = jnp.sum(grad_pre.astype(jnp.float32), axis=0)
    grad_normed2 = jnp.einsum("tf,df->td", grad_pre, full_w1, preferred_element_type=jnp.float32)
    grad_mid_norm, grad_g2, grad_b2 = norm2_back(grad_normed2)
    grad_middle = grad_out_f + grad_mid_norm
    mlp_sums = share_mlp((grad_g2, grad_b2, grad_w1, grad_c1, grad_w2, grad_c2))
    grad_branch = grad_middle.astype(jnp.bfloat16)
    grad_wo = jnp.einsum("td,te->de", attended, grad_branch, preferred_element_type=jnp.float32)
    grad_bo = jnp.sum(grad_branch.astype(jnp.float32), axis=0)
    grad_attended = jnp.einsum(
        "te,de->td", grad_branch, full_wo, preferred_element_type=jnp.float32
    ).astype(jnp.bfloat16)
    grad_attended_heads = lax.all_to_all(
        grad_attended.reshape(shape3), "seq", split_axis=2, concat_axis=1, tiled=True
    )
    grad_q_heads, grad_k_heads, grad_v_heads = lax.map(
        attend_clip_back,
        (query_clips, key_clips, value_clips, grad_attended_heads, log_totals, lengths),
    )
    grad_q, grad_k, grad_v = (
        lax.all_to_all(grad_q_heads, "seq", split_axis=1, concat_axis=2, tiled=True),
        lax.all_to_all(grad_k_heads, "seq", split_axis=1, concat_axis=2, tiled=True),
        lax.all_to_all(grad_v_heads, "seq", split_axis=1, concat_axis=2, tiled=True),
    )
    grad_q = grad_q.reshape(total_rows, width)
    grad_k = grad_k.reshape(total_rows, width)
    grad_v = grad_v.reshape(total_rows, width)
    grad_qkv = jnp.concatenate(
        [
            jnp.einsum("td,te->de", normed, grad_q, preferred_element_type=jnp.float32),
            jnp.einsum("td,te->de", normed, grad_k, preferred_element_type=jnp.float32),
            jnp.einsum("td,te->de", normed, grad_v, preferred_element_type=jnp.float32),
        ],
        axis=1,
    )
    grad_qb = jnp.sum(grad_q.astype(jnp.float32), axis=0)
    grad_vb = jnp.sum(grad_v.astype(jnp.float32), axis=0)
    grad_normed = (
        jnp.einsum("te,de->td", grad_q, full_qkv[:, :width], preferred_element_type=jnp.float32)
        + jnp.einsum(
            "te,de->td", grad_k, full_qkv[:, width : 2 * width], preferred_element_type=jnp.float32
        )
        + jnp.einsum(
            "te,de->td", grad_v, full_qkv[:, 2 * width :], preferred_element_type=jnp.float32
        )
    )
    grad_in_norm, grad_g1, grad_b1 = norm1_back(grad_normed)
    grad_inputs = (grad_middle + grad_in_norm).reshape(shape3)
    attn_sums = share_attn((grad_g1, grad_b1, grad_qkv, grad_qb, grad_vb, grad_wo, grad_bo))
    return (
        layer_out,
        grad_inputs,
        attn_sums[0],
        attn_sums[1],
        attn_sums[2],
        attn_sums[3],
        attn_sums[4],
        attn_sums[5],
        attn_sums[6],
        mlp_sums[0],
        mlp_sums[1],
        mlp_sums[2],
        mlp_sums[3],
        mlp_sums[4],
        mlp_sums[5],
    )


def solution(mesh):
    in_specs = (
        P("fsdp", "seq", None),
        P("fsdp"),
        P("fsdp"),
        P("fsdp"),
        P("fsdp", None),
        P("fsdp"),
        P("fsdp"),
        P("fsdp", None),
        P("fsdp"),
        P("fsdp"),
        P("fsdp"),
        P("fsdp", None),
        P("fsdp"),
        P("fsdp", None),
        P("fsdp"),
        P("fsdp", "seq", None),
    )
    out_specs = (
        P("fsdp", "seq", None),
        P("fsdp", "seq", None),
        P("fsdp"),
        P("fsdp"),
        P("fsdp", None),
        P("fsdp"),
        P("fsdp"),
        P("fsdp", None),
        P("fsdp"),
        P("fsdp"),
        P("fsdp"),
        P("fsdp", None),
        P("fsdp"),
        P("fsdp", None),
        P("fsdp"),
    )
    return jax.shard_map(shards, mesh=mesh, in_specs=in_specs, out_specs=out_specs, check_vma=False)
```

profile of v0, /device:TPU:0, one launch (start us, length us, event | category | flops | bytes accessed | tf_op | source)
XLA Modules:
  0.0 1296.7 jit_solution(4953560270081156990)
XLA Ops:
  9.4 13.5 %all-gather.1 = bf16[8,1,128]{2,1,0:T(2,128)(2,1)S(1)} all-gather(bf16[1,1,128]{2,1,0:T(2,128)(2,1)} %bitcast.368), channel_id=1, replica_groups=mesh['seq'=4,'fsdp'=8] {'fsdp'}, dimensions={0}, use_global_device_ids=true | all-gather | bytes 2304 | tf_op jit(solution)/shard_map/all_gather | solution.py:204
  53.4 23.8 %all-gather.14.cloned.1.call-done = bf16[1024,3072]{1,0:T(8,128)(2,1)} async-done(((bf16[128,3072]{1,0:T(8,128)(2,1)}), bf16[1024,3072]{1,0:T(8,128)(2,1)}) %all-gather.14.cloned.1.call-update) | async-done | bytes 6291472 | tf_op jit(solution)/shard_map/all_gather | solution.py:205
  106.2 16.0 %all-to-all-done = bf16[2,392,1024]{1,0,2:T(2,128)(2,1)S(1)} async-done(((bf16[2,392,1024]{1,0,2:T(2,128)(2,1)}), bf16[2,392,1024]{1,0,2:T(2,128)(2,1)S(1)}, u32[]{:S(2)}, u32[]{:S(2)}) %all-to-all-start) | async-done | bytes 1605664 | tf_op jit(solution)/shard_map/all_to_all | solution.py:230
  132.8 18.6 %all-to-all-done.1 = bf16[2,392,1024]{1,0,2:T(2,128)(2,1)} async-done(((bf16[2,392,1024]{1,0,2:T(2,128)(2,1)}), bf16[2,392,1024]{1,0,2:T(2,128)(2,1)}, u32[]{:S(2)}, u32[]{:S(2)}) %all-to-all-start.1) | async-done | bytes 1605664 | tf_op jit(solution)/shard_map/all_to_all | solution.py:231
  189.9 107.2 %while.86 = (s32[]{:T(128)}, bf16[2,1568,256]{1,2,0:T(8,128)(2,1)}, f32[2,4,2,784]{3,2,1,0:T(2,128)}, bf16[2,1568,256]{1,2,0:T(8,128)(2,1)}, bf16[2,1568,256]{1,...) while((s32[]{:T(128)}, bf16[2,1568,256]{1,2,0:T(8,128)(2,1)}, ...), condition=%wide.region_9.10_spmd, body=%wide.region_2.9_spmd.sunk | while | flops 329506592 | bytes 28406536 | solution.py:234
  196.0 43.6 %while.89 = (s32[]{:T(128)}, bf16[4,2,784,64]{2,1,3,0:T(2,128)(2,1)}, f32[4,2,784]{2,1,0:T(2,128)S(1)}, bf16[4,2,784,64]{3,2,1,0:T(8,128)(2,1)S(1)}, bf16[4,1568...) while((s32[]{:T(128)}, ...), condition=%wide.region_8.8_spmd.clone, body=%wide.region_3.7_spmd.clone.sunk | while | flops 329506592 | bytes 18669576 | solution.py:57
  249.6 43.5 %while.89 = (s32[]{:T(128)}, bf16[4,2,784,64]{2,1,3,0:T(2,128)(2,1)}, f32[4,2,784]{2,1,0:T(2,128)S(1)}, bf16[4,2,784,64]{3,2,1,0:T(8,128)(2,1)S(1)}, bf16[4,1568...) while((s32[]{:T(128)}, ...), condition=%wide.region_8.8_spmd.clone, body=%wide.region_3.7_spmd.clone.sunk | while | flops 329506592 | bytes 18669576 | solution.py:57
  333.6 12.9 all-gather.7
  354.2 13.1 %fusion.60 = f32[784,4096]{1,0:T(8,128)} fusion(bf16[1024,4096]{1,0:T(8,128)(2,1)} %all-gather.18.cloned.1.call-done, f32[784,1024]{1,0:T(8,128)} %copy-done.16, f32[1024]{0:T(1024)S(1)} %bitcast.364, f32[1024]{0:T(1024)S(1)} %bitcast.354, f32[784]{0:T(1024)S(1)} %fusion.58, f32[784]{0:T(1024)S(1)} %broadcast_multiply_fusion), kind=kOutput, calls=%fused_computation.139 | convolution fusion | flops 6580682752 | bytes 24459392 | tf_op jit(solution)/shard_map/dot_general | solution.py:248
  367.3 41.2 %fusion.61 = (bf16[4096]{0:T(1024)(128)(2,1)}, bf16[784,4096]{1,0:T(8,128)(2,1)}, f32[784,4096]{1,0:T(8,128)}) fusion(f32[784,4096]{1,0:T(8,128)} %fusion.60, f32[4096]{0:T(1024)S(1)} %bitcast.346, bf16[784,1024]{1,0:T(8,128)(2,1)S(1)} %bitcast.309, bf16[4096,1024]{1,0:T(8,128)(2,1)} %all-gather.20.cloned.1.call-done), kind=kOutput, calls=%fused_computation.140 | convolution fusion | flops 6814298112 | bytes 42131456 | tf_op jit(solution)/shard_map/td,fd->tf/dot_general | solution.py:261
  433.9 25.3 %all-to-all-done.4 = bf16[2,392,1024]{1,0,2:T(2,128)(2,1)S(1)} async-done(((bf16[2,392,1024]{1,0,2:T(2,128)(2,1)}), bf16[2,392,1024]{1,0,2:T(2,128)(2,1)S(1)}, u32[]{:S(2)}, u32[]{:S(2)}) %all-to-all-start.4) | async-done | bytes 1605664 | tf_op jit(solution)/shard_map/all_to_all | solution.py:275
  470.7 327.6 %while.88 = (s32[]{:T(128)}, bf16[2,1568,256]{1,2,0:T(8,128)(2,1)}, bf16[2,1568,256]{1,2,0:T(8,128)(2,1)}, bf16[2,1568,256]{1,2,0:T(8,128)(2,1)}, bf16[2,1568,25...) while((s32[]{:T(128)}, bf16[2,1568,256]{1,2,0:T(8,128)(2,1)}, ...), condition=%wide.region_20.21_spmd, body=%wide.region_14.20_spmd.sunk | while | flops 799705920 | bytes 110504456 | solution.py:278
  483.2 146.9 %while.90 = (s32[]{:T(128)}, bf16[4,1568,64]{2,1,0:T(8,128)(2,1)}, bf16[4,1568,64]{1,2,0:T(8,128)(2,1)}, bf16[4,1568,64]{1,2,0:T(8,128)(2,1)}, bf16[4,2,784,64]{...) while((s32[]{:T(128)}, bf16[4,1568,64]{2,1,0:T(8,128)(2,1)}, ...), condition=%wide.region_19.19_spmd.clone, body=%wide.region_15.18_spmd.clone.sunk | while | flops 799705920 | bytes 86221976 | solution.py:110
  488.3 27.3 %while.91 = (s32[]{:T(128)}, f32[1568,64]{0,1:T(8,128)S(1)}, f32[1568,64]{0,1:T(8,128)}, bf16[2,784,64]{1,2,0:T(8,128)(2,1)}, pred[1568]{0:T(1024)(128)(4,1)S(1)...) while((s32[]{:T(128)}, f32[1568,64]{0,1:T(8,128)S(1)}, ...), condition=%wide.region_18.17_spmd.clone, body=%wide.region_16.16_spmd.clone.sunk | while | flops 799503616 | bytes 81542256 | solution.py:101
  525.0 27.3 %while.91 = (s32[]{:T(128)}, f32[1568,64]{0,1:T(8,128)S(1)}, f32[1568,64]{0,1:T(8,128)}, bf16[2,784,64]{1,2,0:T(8,128)(2,1)}, pred[1568]{0:T(1024)(128)(4,1)S(1)...) while((s32[]{:T(128)}, f32[1568,64]{0,1:T(8,128)S(1)}, ...), condition=%wide.region_18.17_spmd.clone, body=%wide.region_16.16_spmd.clone.sunk | while | flops 799503616 | bytes 81542256 | solution.py:101
  561.8 27.3 %while.91 = (s32[]{:T(128)}, f32[1568,64]{0,1:T(8,128)S(1)}, f32[1568,64]{0,1:T(8,128)}, bf16[2,784,64]{1,2,0:T(8,128)(2,1)}, pred[1568]{0:T(1024)(128)(4,1)S(1)...) while((s32[]{:T(128)}, f32[1568,64]{0,1:T(8,128)S(1)}, ...), condition=%wide.region_18.17_spmd.clone, body=%wide.region_16.16_spmd.clone.sunk | while | flops 799503616 | bytes 81542256 | solution.py:101
  598.5 27.3 %while.91 = (s32[]{:T(128)}, f32[1568,64]{0,1:T(8,128)S(1)}, f32[1568,64]{0,1:T(8,128)}, bf16[2,784,64]{1,2,0:T(8,128)(2,1)}, pred[1568]{0:T(1024)(128)(4,1)S(1)...) while((s32[]{:T(128)}, f32[1568,64]{0,1:T(8,128)S(1)}, ...), condition=%wide.region_18.17_spmd.clone, body=%wide.region_16.16_spmd.clone.sunk | while | flops 799503616 | bytes 81542256 | solution.py:101
  647.0 146.9 %while.90 = (s32[]{:T(128)}, bf16[4,1568,64]{2,1,0:T(8,128)(2,1)}, bf16[4,1568,64]{1,2,0:T(8,128)(2,1)}, bf16[4,1568,64]{1,2,0:T(8,128)(2,1)}, bf16[4,2,784,64]{...) while((s32[]{:T(128)}, bf16[4,1568,64]{2,1,0:T(8,128)(2,1)}, ...), condition=%wide.region_19.19_spmd.clone, body=%wide.region_15.18_spmd.clone.sunk | while | flops 799705920 | bytes 86221976 | solution.py:110
  652.1 27.3 %while.91 = (s32[]{:T(128)}, f32[1568,64]{0,1:T(8,128)S(1)}, f32[1568,64]{0,1:T(8,128)}, bf16[2,784,64]{1,2,0:T(8,128)(2,1)}, pred[1568]{0:T(1024)(128)(4,1)S(1)...) while((s32[]{:T(128)}, f32[1568,64]{0,1:T(8,128)S(1)}, ...), condition=%wide.region_18.17_spmd.clone, body=%wide.region_16.16_spmd.clone.sunk | while | flops 799503616 | bytes 81542256 | solution.py:101
  688.8 27.3 %while.91 = (s32[]{:T(128)}, f32[1568,64]{0,1:T(8,128)S(1)}, f32[1568,64]{0,1:T(8,128)}, bf16[2,784,64]{1,2,0:T(8,128)(2,1)}, pred[1568]{0:T(1024)(128)(4,1)S(1)...) while((s32[]{:T(128)}, f32[1568,64]{0,1:T(8,128)S(1)}, ...), condition=%wide.region_18.17_spmd.clone, body=%wide.region_16.16_spmd.clone.sunk | while | flops 799503616 | bytes 81542256 | solution.py:101
  725.5 27.3 %while.91 = (s32[]{:T(128)}, f32[1568,64]{0,1:T(8,128)S(1)}, f32[1568,64]{0,1:T(8,128)}, bf16[2,784,64]{1,2,0:T(8,128)(2,1)}, pred[1568]{0:T(1024)(128)(4,1)S(1)...) while((s32[]{:T(128)}, f32[1568,64]{0,1:T(8,128)S(1)}, ...), condition=%wide.region_18.17_spmd.clone, body=%wide.region_16.16_spmd.clone.sunk | while | flops 799503616 | bytes 81542256 | solution.py:101
  762.3 27.3 %while.91 = (s32[]{:T(128)}, f32[1568,64]{0,1:T(8,128)S(1)}, f32[1568,64]{0,1:T(8,128)}, bf16[2,784,64]{1,2,0:T(8,128)(2,1)}, pred[1568]{0:T(1024)(128)(4,1)S(1)...) while((s32[]{:T(128)}, f32[1568,64]{0,1:T(8,128)S(1)}, ...), condition=%wide.region_18.17_spmd.clone, body=%wide.region_16.16_spmd.clone.sunk | while | flops 799503616 | bytes 81542256 | solution.py:101
  812.7 13.7 %all-to-all-done.7 = bf16[2,1568,256]{2,0,1:T(2,128)(2,1)S(1)} async-done(((bf16[2,1568,256]{2,0,1:T(2,128)(2,1)}), bf16[2,1568,256]{2,0,1:T(2,128)(2,1)S(1)}, u32[]{:S(2)}, u32[]{:S(2)}) %all-to-all-start.7) | async-done | bytes 1605664 | tf_op jit(solution)/shard_map/all_to_all | solution.py:285
  834.4 15.5 %all-to-all-done.6 = bf16[2,1568,256]{2,0,1:T(2,128)(2,1)} async-done(((bf16[2,1568,256]{2,0,1:T(2,128)(2,1)}), bf16[2,1568,256]{2,0,1:T(2,128)(2,1)}, u32[]{:S(2)}, u32[]{:S(2)}) %all-to-all-start.6) | async-done | bytes 1605664 | tf_op jit(solution)/shard_map/all_to_all | solution.py:284
  884.3 13.4 %pad_maximum_fusion = bf16[1024,3072]{0,1:T(8,128)(2,1)} fusion(bf16[1024,1024]{0,1:T(8,128)(2,1)S(1)} %convolution_convert_fusion.4, bf16[1024,1024]{0,1:T(8,128)(2,1)S(1)} %convolution_convert_fusion.5, bf16[1024,1024]{0,1:T(8,128)(2,1)S(1)} %convolution_convert_fusion.6), kind=kLoop, calls=%fused_computation.89 | loop fusion | flops 18874368 | bytes 12582912 | tf_op jit(solution)/shard_map/concatenate | solution.py:290
  913.0 14.7 %convolution_convert_fusion.1 = bf16[1024,4096]{1,0:T(8,128)(2,1)} fusion(bf16[784,4096]{1,0:T(8,128)(2,1)} %get-tuple-element.729, f32[784,1024]{1,0:T(8,128)} %copy-done.16, f32[1024]{0:T(1024)S(1)} %bitcast.365, f32[1024]{0:T(1024)S(1)} %bitcast.357, f32[784]{0:T(1024)S(1)} %copy-done.59, f32[784]{0:T(1024)S(1)} %copy-done.44), kind=kOutput, calls=%fused_computation.87 | convolution fusion | flops 6584877056 | bytes 18036864 | tf_op jit(solution)/shard_map/td,tf->df/dot_general | solution.py:263
  964.5 12.8 add_convert_fusion.2
  981.7 29.1 %reduce-scatter.7.cloned.1.call-done = bf16[128,1024]{1,0:T(8,128)(2,1)} async-done(((bf16[1024,1024]{1,0:T(8,128)(2,1)}), bf16[128,1024]{1,0:T(8,128)(2,1)}) %reduce-scatter.7.cloned.1.call-update) | async-done | bytes 262160 | tf_op jit(solution)/shard_map/reduce_scatter | solution.py:164
  1010.9 90.6 %reduce-scatter.9.cloned.1.call-done = bf16[128,4096]{1,0:T(8,128)(2,1)} async-done(((bf16[1024,4096]{1,0:T(8,128)(2,1)}), bf16[128,4096]{1,0:T(8,128)(2,1)}) %reduce-scatter.9.cloned.1.call-update) | async-done | bytes 1048592 | tf_op jit(solution)/shard_map/reduce_scatter | solution.py:124
  1101.5 90.3 %reduce-scatter.11.cloned.1.call-done = bf16[512,1024]{1,0:T(8,128)(2,1)} async-done(((bf16[4096,1024]{1,0:T(8,128)(2,1)}), bf16[512,1024]{1,0:T(8,128)(2,1)}) %reduce-scatter.11.cloned.1.call-update) | async-done | bytes 1048592 | tf_op jit(solution)/shard_map/reduce_scatter | solution.py:130
  1205.7 26.0 %all-reduce.9 = (bf16[1024]{0:T(1024)(128)(2,1)S(1)}, bf16[1024]{0:T(1024)(128)(2,1)S(1)}, bf16[1024]{0:T(1024)(128)(2,1)S(1)}, bf16[1024]{0:T(1024)(128)(2,1)S(...) all-reduce(bf16[1024]{0:T(1024)(128)(2,1)S(1)} %get-tuple-element.6, ...), channel_id=2, replica_groups=mesh['seq'=4,'fsdp'=8] {'fsdp'}, use_global_device_ids=true, to_apply=%region_24.25.clone | all-reduce | flops 12288 | bytes 49152
  1259.0 23.3 %all-reduce.14.cloned.1.call-done = (bf16[128,3072]{0,1:T(8,128)(2,1)}, bf16[128,1024]{1,0:T(8,128)(2,1)}, bf16[128,4096]{1,0:T(8,128)(2,1)}, bf16[512,1024]{1,0:T(8,128)(2,1)}) async-done(((bf16[128,3072]{0,1:T(8,128)(2,1)}, bf16[128,1024]{1,0:T(8,128)(2,1)}, bf16[128,4096]{1,0:T(8,128)(2,1)}, bf16[512,1024]{1,0:T(8,128)(2,1)}), (bf16[128,3072]{0,1:T(8,128)(2,1)}, bf16[128,1024]{1,0:T(8,128)(2,1)}, ...) | async-done | bytes 3145744 | tf_op jit(solution)/shard_map/psum | solution.py:174
  (868 shorter events, 845.2 us)
Async XLA Ops:
  7.2 37.5 %copy-start.68 = (bf16[128]{0:T(256)(128)(2,1)S(1)}, bf16[128]{0:T(256)(128)(2,1)}, u32[]{:S(2)}) copy-start(bf16[128]{0:T(256)(128)(2,1)} %param.33) | copy-start | bytes 772
  7.2 70.0 %all-gather.14.cloned.1.call-start = ((), (), s32[]{:S(2)}) async-start(), calls=%async_computation.12 | async-start | bytes 7077888 | tf_op jit(solution)/shard_map/all_gather | solution.py:205
  7.9 339.9 %all-gather.16.cloned.1.call-start = ((), (), s32[]{:S(2)}) async-start(), calls=%async_computation.13 | async-start | bytes 2359296 | tf_op jit(solution)/shard_map/all_gather | solution.py:208
  8.7 345.4 %all-gather.18.cloned.1.call-start = ((), (), s32[]{:S(2)}) async-start(), calls=%async_computation.14 | async-start | bytes 9437184 | tf_op jit(solution)/shard_map/all_gather | solution.py:214
  23.0 61.7 %copy-start.54 = (f32[8,1,128]{2,1,0:T(1,128)}, f32[8,1,128]{2,1,0:T(1,128)S(1)}, u32[]{:S(2)}) copy-start(f32[8,1,128]{2,1,0:T(1,128)S(1)} %convert_element_type.228) | copy-start | bytes 12292
  31.8 52.9 %copy-start.39 = (f32[8,1,128]{2,1,0:T(1,128)}, f32[8,1,128]{2,1,0:T(1,128)S(1)}, u32[]{:S(2)}) copy-start(f32[8,1,128]{2,1,0:T(1,128)S(1)} %convert_element_type.227) | copy-start | bytes 12292
  32.1 52.6 %copy-start.37 = (f32[2,392]{1,0:T(2,128)}, f32[2,392]{1,0:T(2,128)S(1)}, u32[]{:S(2)}) copy-start(f32[2,392]{1,0:T(2,128)S(1)} %broadcast_multiply_fusion.1) | copy-start | bytes 9412
  32.2 52.5 %copy-start.50 = (f32[784]{0:T(1024)}, f32[784]{0:T(1024)S(1)}, u32[]{:S(2)}) copy-start(f32[784]{0:T(1024)S(1)} %div.47) | copy-start | bytes 9412
  33.5 51.2 %copy-start.47 = (f32[784]{0:T(1024)}, f32[784]{0:T(1024)S(1)}, u32[]{:S(2)}) copy-start(f32[784]{0:T(1024)S(1)} %add.197) | copy-start | bytes 9412
  33.5 51.2 %copy-start.52 = (f32[784]{0:T(1024)}, f32[784]{0:T(1024)S(1)}, u32[]{:S(2)}) copy-start(f32[784]{0:T(1024)S(1)} %rsqrt.23) | copy-start | bytes 9412
  93.0 29.2 %all-to-all-start = ((bf16[2,392,1024]{1,0,2:T(2,128)(2,1)}), bf16[2,392,1024]{1,0,2:T(2,128)(2,1)S(1)}, u32[]{:S(2)}, u32[]{:S(2)}) async-start(bf16[2,392,1024]{1,0,2:T(2,128)(2,1)} %copy.137), calls=%async_computation | async-start | bytes 4194304 | tf_op jit(solution)/shard_map/all_to_all | solution.py:230
  122.2 29.3 %all-to-all-start.1 = ((bf16[2,392,1024]{1,0,2:T(2,128)(2,1)}), bf16[2,392,1024]{1,0,2:T(2,128)(2,1)}, u32[]{:S(2)}, u32[]{:S(2)}) async-start(bf16[2,392,1024]{1,0,2:T(2,128)(2,1)} %copy.140), calls=%async_computation.1 | async-start | bytes 4194304 | tf_op jit(solution)/shard_map/all_to_all | solution.py:231
  151.5 28.8 %all-to-all-start.2 = ((bf16[2,392,1024]{1,0,2:T(2,128)(2,1)}), bf16[2,392,1024]{1,0,2:T(2,128)(2,1)}, u32[]{:S(2)}, u32[]{:S(2)}) async-start(bf16[2,392,1024]{1,0,2:T(2,128)(2,1)} %copy.143), calls=%async_computation.2 | async-start | bytes 4194304 | tf_op jit(solution)/shard_map/all_to_all | solution.py:232
  155.9 211.4 %all-gather.20.cloned.1.call-start = ((), (), s32[]{:S(2)}) async-start(), calls=%async_computation.15 | async-start | bytes 9437184 | tf_op jit(solution)/shard_map/all_gather | solution.py:216
  297.1 36.5 %copy-start.66 = (bf16[512]{0:T(512)(128)(2,1)S(1)}, bf16[512]{0:T(512)(128)(2,1)}, u32[]{:S(2)}) copy-start(bf16[512]{0:T(512)(128)(2,1)} %param.40) | copy-start | bytes 3076
  302.5 44.0 %all-to-all-start.3 = ((bf16[2,1568,256]{2,0,1:T(2,128)(2,1)}), bf16[2,1568,256]{2,0,1:T(2,128)(2,1)S(1)}, u32[]{:S(2)}, u32[]{:S(2)}) async-start(bf16[2,1568,256]{2,0,1:T(2,128)(2,1)} %copy.149), calls=%async_computation.3 | async-start | bytes 3211264 | tf_op jit(solution)/shard_map/all_to_all | solution.py:237
  333.6 85.9 %copy-start.56 = (f32[8,1,128]{2,1,0:T(1,128)}, f32[8,1,128]{2,1,0:T(1,128)S(1)}, u32[]{:S(2)}) copy-start(f32[8,1,128]{2,1,0:T(1,128)S(1)} %convert_element_type.232) | copy-start | bytes 12292
  351.9 67.5 %copy-start.43 = (f32[784]{0:T(1024)}, f32[784]{0:T(1024)S(1)}, u32[]{:S(2)}) copy-start(f32[784]{0:T(1024)S(1)} %broadcast_multiply_fusion) | copy-start | bytes 9412
  354.1 65.4 %copy-start.58 = (f32[784]{0:T(1024)}, f32[784]{0:T(1024)S(1)}, u32[]{:S(2)}) copy-start(f32[784]{0:T(1024)S(1)} %fusion.58) | copy-start | bytes 9412
  367.3 41.2 %copy-start.17 = (f32[784,1024]{1,0:T(8,128)S(1)}, f32[784,1024]{1,0:T(8,128)}, u32[]{:S(2)}) copy-start(f32[784,1024]{1,0:T(8,128)} %copy-done.16) | copy-start | bytes 9633796
  367.3 41.2 %copy-start.73 = (bf16[1024,4096]{1,0:T(8,128)(2,1)S(1)}, bf16[1024,4096]{1,0:T(8,128)(2,1)}, u32[]{:S(2)}) copy-start(bf16[1024,4096]{1,0:T(8,128)(2,1)} %all-gather.18.cloned.1.call-done) | copy-start | bytes 25165828
  429.6 29.6 %all-to-all-start.4 = ((bf16[2,392,1024]{1,0,2:T(2,128)(2,1)}), bf16[2,392,1024]{1,0,2:T(2,128)(2,1)S(1)}, u32[]{:S(2)}, u32[]{:S(2)}) async-start(bf16[2,392,1024]{1,0,2:T(2,128)(2,1)} %copy.152), calls=%async_computation.4 | async-start | bytes 4194304 | tf_op jit(solution)/shard_map/all_to_all | solution.py:275
  803.6 22.8 %all-to-all-start.7 = ((bf16[2,1568,256]{2,0,1:T(2,128)(2,1)}), bf16[2,1568,256]{2,0,1:T(2,128)(2,1)S(1)}, u32[]{:S(2)}, u32[]{:S(2)}) async-start(bf16[2,1568,256]{2,0,1:T(2,128)(2,1)} %copy.165), calls=%async_computation.7 | async-start | bytes 3211264 | tf_op jit(solution)/shard_map/all_to_all | solution.py:285
  826.4 23.5 %all-to-all-start.6 = ((bf16[2,1568,256]{2,0,1:T(2,128)(2,1)}), bf16[2,1568,256]{2,0,1:T(2,128)(2,1)}, u32[]{:S(2)}, u32[]{:S(2)}) async-start(bf16[2,1568,256]{2,0,1:T(2,128)(2,1)} %copy.162), calls=%async_computation.6 | async-start | bytes 3211264 | tf_op jit(solution)/shard_map/all_to_all | solution.py:284
  849.9 23.5 %all-to-all-start.5 = ((bf16[2,1568,256]{2,0,1:T(2,128)(2,1)}), bf16[2,1568,256]{2,0,1:T(2,128)(2,1)}, u32[]{:S(2)}, u32[]{:S(2)}) async-start(bf16[2,1568,256]{2,0,1:T(2,128)(2,1)} %copy.159), calls=%async_computation.5 | async-start | bytes 3211264 | tf_op jit(solution)/shard_map/all_to_all | solution.py:283
  854.2 125.1 %reduce-scatter.13.cloned.1.call-start = ((), (), s32[]{:S(2)}) async-start(), calls=%async_computation.19 | async-start | bytes 7077888
  906.4 104.4 %reduce-scatter.7.cloned.1.call-start = ((), (), s32[]{:S(2)}) async-start(), calls=%async_computation.16 | async-start | bytes 2359296 | tf_op jit(solution)/shard_map/reduce_scatter | solution.py:164
  912.9 188.6 %reduce-scatter.9.cloned.1.call-start = ((), (), s32[]{:S(2)}) async-start(), calls=%async_computation.17 | async-start | bytes 9437184 | tf_op jit(solution)/shard_map/reduce_scatter | solution.py:124
  927.8 264.0 %reduce-scatter.11.cloned.1.call-start = ((), (), s32[]{:S(2)}) async-start(), calls=%async_computation.18 | async-start | bytes 9437184 | tf_op jit(solution)/shard_map/reduce_scatter | solution.py:130
  952.3 330.1 %all-reduce.14.cloned.1.call-start = ((), (), s32[]{:S(2)}) async-start(), calls=%async_computation.20 | async-start | bytes 6291456 | tf_op jit(solution)/shard_map/psum | solution.py:174
  979.3 212.5 %copy-start.27 = (bf16[98,8,4,256]{3,1,2,0:T(8,128)(2,1)S(1)}, bf16[98,8,4,256]{3,1,2,0:T(8,128)(2,1)}, u32[]{:S(2)}) copy-start(bf16[98,8,4,256]{3,1,2,0:T(8,128)(2,1)} %copy-done.26) | copy-start | bytes 4816900
  1199.1 48.0 %copy-start.48 = (f32[784]{0:T(1024)S(1)}, f32[784]{0:T(1024)}, u32[]{:S(2)}) copy-start(f32[784]{0:T(1024)} %copy-done.47) | copy-start | bytes 9412
  (123 other events, 692.9 us)
Sparse Core Ops, SparseCore 0:
  9.7 67.5 all-gather.13
  78.8 27.7 all-gather.15
  108.2 81.5 all-gather.17
  191.3 80.5 all-gather.19
  906.5 67.4 reduce-scatter.12
  976.7 34.1 reduce-scatter.6
  1013.2 88.3 reduce-scatter.8
  1103.8 87.9 reduce-scatter.10
  1195.7 86.5 all-reduce.13
where the time goes:
time: 1310 us; the launch traced here: 1300 us
  waiting for transfers between devices  367 us (28%)
  matrix products  342 us (26%)
  local copies, waits for them, and re-layouts  291 us (22%)
  blocking collectives  128 us (10%)
  other arithmetic  117 us (9%)
  starting transfers between devices  33.7 us (3%)
  between operations  16.4 us (1%)
    reduce_scatter x1, waiting for transfers between devices, share_mlp(): lax.psum_scatter(terms[2].astype(jnp.bfloat16), 'fsdp', scatter_dimension...  90.6 us
    reduce_scatter x1, waiting for transfers between devices, share_mlp(): lax.psum_scatter(terms[4].astype(jnp.bfloat16), 'fsdp', scatter_dimension...  90.3 us
    dot_general x32, matrix products, per_block(): jnp.einsum('qd,kd->qk', query_rows, head_keys, preferred_element_type=jnp...  59.9 us
    while x142, local copies, waits for them, and re-layouts  54.1 us
    dot_general x1, matrix products, shards(): jnp.einsum('td,fd->tf', grad_out, full_w2, preferred_element_type=jnp.flo...  41.2 us
    dot_general x16, matrix products, per_block(): jnp.einsum('qk,qd->kd', probs.astype(jnp.bfloat16), grad_rows, preferred_...  38.9 us
    dot_general x16, matrix products, per_block(): jnp.einsum('qd,kd->qk', grad_rows, head_values, preferred_element_type=jn...  31.3 us
    dynamic_slice x48, local copies, waits for them, and re-layouts, attend_clip(): lax.map(per_head, (query_heads, key_heads, value_heads))  30.9 us
  transfers between devices with their start and end apart: 17, of which 12 were waited for; matrix products, arithmetic and copies ran while one was open for 23% of the time, Pallas kernels for 0%

commit v1 on v0

v1 whole, which is shorter than its diff:
```python
import functools

import jax
import jax.numpy as jnp
from jax import lax
from jax.experimental import pallas as pl
from jax.experimental.pallas import tpu as pltpu
from jax.sharding import PartitionSpec as P

HEAD_DIM = 64
PAIR = 2 * HEAD_DIM
EPSILON = 1e-06
NEGATIVE = -1e30
F32, BF16 = jnp.float32, jnp.bfloat16
SCALE = HEAD_DIM ** -0.5
SCALE2 = SCALE * 1.4426950408889634
NT = (((1,), (1,)), ((), ()))
NN = (((1,), (0,)), ((), ()))
TN = (((0,), (0,)), ((), ()))


def dot(a, b, dims=NN):
    return lax.dot_general(a, b, dims, preferred_element_type=F32)


def of_head(block, h):
    lane = lax.broadcasted_iota(jnp.int32, (1, PAIR), 1)
    return jnp.where(lane // HEAD_DIM == h, block, jnp.zeros_like(block))


def valid_rows(j, bk, length):
    return j * bk + lax.broadcasted_iota(jnp.int32, (bk, 1), 0) < length


def transposed_chunks(out_ref, in_ref, cols, bk):
    for j in range(in_ref.shape[1] // bk):
        out_ref[j] = jnp.transpose(in_ref[0, pl.ds(j * bk, bk), cols])


def attend_kernel(len_ref, q_ref, k_ref, v_ref, o_ref, lse_ref, s_ref, vt_ref, ot_ref, *, bk):
    length = len_ref[pl.program_id(0)]
    rows_all, width = q_ref.shape[1:]
    chunks = pl.cdiv(length, bk)
    for pair in range(width // PAIR):
        cols = pl.ds(PAIR * pair, PAIR)
        transposed_chunks(vt_ref, v_ref, cols, bk)
        queries = [of_head(q_ref[0, :, cols], h) for h in range(2)]

        def score(j, tops):
            keys = k_ref[0, pl.ds(pl.multiple_of(j * bk, bk), bk), cols]
            ok = valid_rows(j, bk, length)
            out = []
            for h in range(2):
                s = jnp.where(ok, dot(keys, queries[h], NT), NEGATIVE)
                s_ref[h, j] = s
                top = tops[h]
                for i in range(bk // 8):
                    top = jnp.maximum(top, s[8 * i : 8 * i + 8])
                out.append(top)
            return tuple(out)

        low = jnp.full((8, rows_all), NEGATIVE, F32)
        tops = lax.fori_loop(0, chunks, score, (low, low))
        peaks = [jnp.max(top, axis=0, keepdims=True) * SCALE2 for top in tops]
        ot_ref[...] = jnp.zeros_like(ot_ref)

        def mix(j, sums):
            out = []
            for h in range(2):
                p = jnp.exp2(s_ref[h, j] * SCALE2 - peaks[h])
                total = sums[h]
                for i in range(bk // 8):
                    total = total + p[8 * i : 8 * i + 8]
                out.append(total)
                half = pl.ds(HEAD_DIM * h, HEAD_DIM)
                ot_ref[half] += dot(vt_ref[j, half], p.astype(BF16))
            return tuple(out)

        zero = jnp.zeros((8, rows_all), F32)
        sums = lax.fori_loop(0, chunks, mix, (zero, zero))
        for h in range(2):
            total = jnp.sum(sums[h], axis=0, keepdims=True)
            half = pl.ds(HEAD_DIM * h, HEAD_DIM)
            lse_ref[0, pl.ds(2 * pair + h, 1)] = peaks[h] + jnp.log2(total)
            ot_ref[half] = ot_ref[half] / total
        o_ref[0, :, cols] = jnp.transpose(ot_ref[...]).astype(BF16)


def attend_back_kernel(
    len_ref, q_ref, k_ref, v_ref, do_ref, o_ref, lse_ref, d_ref, kt_ref, dqt_ref, *, bk
):
    length = len_ref[pl.program_id(0)]
    width = q_ref.shape[2]
    chunks = pl.cdiv(length, bk)
    d_ref[...] = jnp.zeros_like(d_ref)
    for pair in range(width // PAIR):
        cols = pl.ds(PAIR * pair, PAIR)
        outs = do_ref[0, :, cols]
        both = jnp.transpose(outs.astype(F32) * o_ref[0, :, cols].astype(F32))
        inner = [
            jnp.sum(both[HEAD_DIM * h : HEAD_DIM * (h + 1)], axis=0, keepdims=True)
            for h in range(2)
        ]
        queries = [of_head(q_ref[0, :, cols], h) for h in range(2)]
        grads = [of_head(outs, h) for h in range(2)]
        logs = [lse_ref[0, pl.ds(2 * pair + h, 1)] for h in range(2)]
        transposed_chunks(kt_ref, k_ref, cols, bk)
        dqt_ref[...] = jnp.zeros_like(dqt_ref)

        def step(j, carry):
            rows = pl.ds(pl.multiple_of(j * bk, bk), bk)
            keys = k_ref[0, rows, cols]
            values = v_ref[0, rows, cols]
            ok = valid_rows(j, bk, length)
            dk = jnp.zeros((bk, PAIR), F32)
            dv = jnp.zeros((bk, PAIR), F32)
            for h in range(2):
                p = jnp.exp2(dot(keys, queries[h], NT) * SCALE2 - logs[h])
                p = jnp.where(ok, p, 0.0)
                g = (p * (dot(values, grads[h], NT) - inner[h])).astype(BF16)
                dv = dv + dot(p.astype(BF16), grads[h])
                dk = dk + dot(g, queries[h])
                half = pl.ds(HEAD_DIM * h, HEAD_DIM)
                dqt_ref[half] += dot(kt_ref[j, half], g)
            d_ref[0, rows, pl.ds(width + PAIR * pair, PAIR)] = (dk * SCALE).astype(BF16)
            d_ref[0, rows, pl.ds(2 * width + PAIR * pair, PAIR)] = dv.astype(BF16)
            return carry

        lax.fori_loop(0, chunks, step, 0)
        d_ref[0, :, cols] = jnp.transpose(dqt_ref[...] * SCALE).astype(BF16)


def chunk_rows(rows):
    return max(b for b in range(8, 225, 8) if rows % b == 0)


def block(rows, width, at):
    return pl.BlockSpec((1, rows, width), lambda c, n: (c, 0, at))


def attend(qkv, lengths):
    clips, rows, triple = qkv.shape
    width = triple // 3
    heads, bk = width // HEAD_DIM, chunk_rows(rows)
    cost = clips * heads * rows * rows
    return pl.pallas_call(
        functools.partial(attend_kernel, bk=bk),
        grid_spec=pltpu.PrefetchScalarGridSpec(
            num_scalar_prefetch=1,
            grid=(clips,),
            in_specs=[block(rows, width, i) for i in range(3)],
            out_specs=[block(rows, width, 0), block(heads, rows, 0)],
            scratch_shapes=[
                pltpu.VMEM((2, rows // bk, bk, rows), F32),
                pltpu.VMEM((rows // bk, PAIR, bk), BF16),
                pltpu.VMEM((PAIR, rows), F32),
            ],
        ),
        out_shape=[
            jax.ShapeDtypeStruct((clips, rows, width), BF16),
            jax.ShapeDtypeStruct((clips, heads, rows), F32),
        ],
        compiler_params=pltpu.CompilerParams(vmem_limit_bytes=40 << 20),
        cost_estimate=pl.CostEstimate(
            flops=cost * 1024, bytes_accessed=clips * rows * width * 8, transcendentals=cost
        ),
        name="attend",
    )(lengths, qkv, qkv, qkv)


def attend_back(qkv, grads, outs, logs, lengths):
    clips, rows, triple = qkv.shape
    width = triple // 3
    heads, bk = width // HEAD_DIM, chunk_rows(rows)
    cost = clips * heads * rows * rows
    return pl.pallas_call(
        functools.partial(attend_back_kernel, bk=bk),
        grid_spec=pltpu.PrefetchScalarGridSpec(
            num_scalar_prefetch=1,
            grid=(clips,),
            in_specs=[block(rows, width, i) for i in (0, 1, 2, 0, 0)] + [block(heads, rows, 0)],
            out_specs=block(rows, triple, 0),
            scratch_shapes=[
                pltpu.VMEM((rows // bk, PAIR, bk), BF16),
                pltpu.VMEM((PAIR, rows), F32),
            ],
        ),
        out_shape=jax.ShapeDtypeStruct((clips, rows, triple), BF16),
        compiler_params=pltpu.CompilerParams(vmem_limit_bytes=40 << 20),
        cost_estimate=pl.CostEstimate(
            flops=cost * 2560, bytes_accessed=clips * rows * width * 16, transcendentals=cost
        ),
        name="attend_back",
    )(lengths, qkv, qkv, qkv, grads, outs, logs)


def swap(value, ring, r):
    return lax.ppermute(value, "seq", [(i, i ^ r) for i in range(ring)])


def gather_seq(value, ring, me):
    out = jnp.zeros((ring,) + value.shape, value.dtype)
    out = lax.dynamic_update_index_in_dim(out, value, me, 0)
    for r in range(1, ring):
        out = lax.dynamic_update_index_in_dim(out, swap(value, ring, r), me ^ r, 0)
    return out


def sum_seq(terms, ring, me):
    total = lax.dynamic_index_in_dim(terms, me, 0, keepdims=False).astype(F32)
    for r in range(1, ring):
        term = lax.dynamic_index_in_dim(terms, me ^ r, 0, keepdims=False)
        total = total + swap(term, ring, r).astype(F32)
    return total


def sum_owned(grad, ring, me):
    owned = lax.psum_scatter(grad.astype(BF16), "fsdp", scatter_dimension=0, tiled=True)
    rows, width = owned.shape
    part = sum_seq(owned.reshape(ring, rows // ring, width), ring, me).astype(BF16)
    return gather_seq(part, ring, me).reshape(rows, width).astype(F32)


def normalize(values):
    centered = values - jnp.mean(values, axis=-1, keepdims=True)
    variance = jnp.mean(centered * centered, axis=-1, keepdims=True)
    rstd = lax.rsqrt(variance + EPSILON)
    return centered * rstd, rstd


def normalize_back(grad, normed, rstd, gain):
    e = grad * gain
    mean = jnp.mean(e, axis=-1, keepdims=True)
    along = jnp.mean(e * normed, axis=-1, keepdims=True)
    return rstd * (e - mean - normed * along)


def shards(
    ring,
    tokens,
    lengths,
    ln1_gain,
    ln1_bias,
    w_qkv,
    q_bias,
    v_bias,
    w_out,
    b_out,
    ln2_gain,
    ln2_bias,
    w_fc1,
    b_fc1,
    w_fc2,
    b_fc2,
    cotangent,
):
    clips, rows, width = tokens.shape
    total_rows = clips * rows
    clip_rows = rows * ring
    local = width // ring
    me = lax.axis_index("seq")

    whole = [gather_seq(tokens[c], ring, me).reshape(clip_rows, width) for c in range(clips)]

    own = ln1_gain.shape[0]
    packed = jnp.concatenate(
        [
            jnp.stack([ln1_gain, ln1_bias, q_bias, v_bias, b_out, ln2_gain, ln2_bias, b_fc2]),
            b_fc1.reshape(-1, own),
        ]
    )
    vectors = lax.all_gather(packed, "fsdp", axis=0, tiled=False)
    c1 = vectors[:, 8:].reshape(-1).astype(F32)
    vectors = vectors[:, :8].transpose(1, 0, 2).reshape(8, width).astype(F32)
    g1, b1, qb, vb, bo, g2, b2, c2 = (vectors[i] for i in range(8))
    qb_mine = lax.dynamic_slice_in_dim(qb, me * local, local)
    vb_mine = lax.dynamic_slice_in_dim(vb, me * local, local)
    bias_mine = jnp.concatenate([qb_mine, jnp.zeros_like(qb_mine), vb_mine])

    mine = lax.dynamic_index_in_dim(w_qkv.reshape(own, 3, ring, local), me, 2, keepdims=False)
    wqkv = lax.all_gather(mine.reshape(own, 3 * local), "fsdp", axis=0, tiled=True)
    wo = lax.all_gather(w_out, "fsdp", axis=0, tiled=True)
    w1 = lax.all_gather(w_fc1, "fsdp", axis=0, tiled=True)
    w2 = lax.all_gather(w_fc2, "fsdp", axis=0, tiled=True)

    normed, qkv, heads_out, logs, attended = [], [], [], [], []
    for c in range(clips):
        n1 = normalize(whole[c].astype(F32))[0]
        h1 = (n1 * g1 + b1).astype(BF16)
        part = (dot(h1, wqkv) + bias_mine).astype(BF16)[None]
        out, log = attend(part, lax.dynamic_slice_in_dim(lengths, c, 1))
        moved = lax.all_to_all(
            out.reshape(ring, rows, local), "seq", split_axis=0, concat_axis=0, tiled=True
        )
        normed.append(h1)
        qkv.append(part)
        heads_out.append(out)
        logs.append(log)
        attended.append(moved.transpose(1, 0, 2).reshape(rows, width))
    attended = jnp.concatenate(attended, axis=0)

    inputs = tokens.astype(F32).reshape(total_rows, width)
    middle = inputs + (dot(attended, wo) + bo)
    n2, r2 = normalize(middle)
    h2 = (n2 * g2 + b2).astype(BF16)
    z = dot(h2, w1) + c1
    phi = 0.5 * (1.0 + lax.erf(z * (2.0 ** -0.5)))
    hidden = (z * phi).astype(BF16)
    slope = phi + z * (jnp.exp(-0.5 * z * z) * 0.3989422804014327)
    layer_out = (middle + (dot(hidden, w2) + c2)).astype(BF16).reshape(clips, rows, width)

    dy = cotangent.reshape(total_rows, width)
    dy_f = dy.astype(F32)
    grad_w2 = sum_owned(dot(hidden, dy, TN), ring, me)
    dz = (dot(dy, w2, NT) * slope).astype(BF16)
    grad_w1 = sum_owned(dot(h2, dz, TN), ring, me)
    dh2 = dot(dz, w1, NT)
    grad_middle = dy_f + normalize_back(dh2, n2, r2, g2)
    da = grad_middle.astype(BF16)
    grad_wo = sum_owned(dot(attended, da, TN), ring, me)
    do = dot(da, wo, NT).astype(BF16)

    dqkv, own_terms, gain_sum, shift_sum = [], [], 0.0, 0.0
    for c in range(clips):
        sent = do[c * rows : (c + 1) * rows].reshape(rows, ring, local).transpose(1, 0, 2)
        moved = lax.all_to_all(sent, "seq", split_axis=0, concat_axis=0, tiled=True)
        moved = moved.reshape(1, clip_rows, local)
        d = attend_back(
            qkv[c], moved, heads_out[c], logs[c], lax.dynamic_slice_in_dim(lengths, c, 1)
        )[0]
        dh1 = dot(d, wqkv, NT)
        n1 = normalize(whole[c].astype(F32))[0]
        gain_sum = gain_sum + jnp.sum(dh1 * n1, axis=0)
        shift_sum = shift_sum + jnp.sum(dh1, axis=0)
        own_terms.append(sum_seq(dh1.astype(BF16).reshape(ring, rows, width), ring, me))
        dqkv.append(d)
    dqkv = jnp.concatenate(dqkv, axis=0)
    grad_mine = dot(jnp.concatenate(normed, axis=0), dqkv, TN)
    owned = lax.psum_scatter(grad_mine.astype(BF16), "fsdp", scatter_dimension=0, tiled=True)
    grad_qkv = gather_seq(owned.reshape(own, 3, local), ring, me)
    grad_qkv = grad_qkv.transpose(1, 2, 0, 3).reshape(own, 3 * width).astype(F32)

    bias_sum = jnp.sum(dqkv.astype(F32), axis=0)
    zeros = jnp.zeros((width,), F32)
    first = jnp.stack(
        [
            gain_sum,
            shift_sum,
            lax.dynamic_update_slice_in_dim(zeros, bias_sum[:local], me * local, 0),
            lax.dynamic_update_slice_in_dim(zeros, bias_sum[2 * local :], me * local, 0),
        ]
    )
    second = jnp.stack(
        [
            jnp.sum(dh2 * n2, axis=0),
            jnp.sum(dh2, axis=0),
            jnp.sum(dy_f, axis=0),
            jnp.sum(da.astype(F32), axis=0),
        ]
    )
    second = jnp.concatenate([second, jnp.sum(dz.astype(F32), axis=0).reshape(-1, width)])
    at = lax.axis_index("fsdp") * own
    small = lax.psum(second.astype(BF16), ("seq", "fsdp")).astype(F32)
    four = lax.dynamic_slice_in_dim(small[:4], at, own, axis=1)
    grad_c1 = lax.dynamic_slice_in_dim(
        small[4:].reshape(-1), lax.axis_index("fsdp") * b_fc1.shape[0], b_fc1.shape[0]
    )
    late = lax.psum(first.astype(BF16), ("seq", "fsdp")).astype(F32)
    late = lax.dynamic_slice_in_dim(late, at, own, axis=1)

    terms = jnp.concatenate(own_terms, axis=0)
    n1, r1 = normalize(inputs)
    grad_inputs = (grad_middle + normalize_back(terms, n1, r1, g1)).reshape(clips, rows, width)
    return (
        layer_out,
        grad_inputs,
        late[0],
        late[1],
        grad_qkv,
        late[2],
        late[3],
        grad_wo,
        four[3],
        four[0],
        four[1],
        grad_w1,
        grad_c1,
        grad_w2,
        four[2],
    )


def solution(mesh):
    act, vec, mat = P("fsdp", "seq", None), P("fsdp"), P("fsdp", None)
    in_specs = (act, vec, vec, vec, mat, vec, vec, mat, vec, vec, vec, mat, vec, mat, vec, act)
    out_specs = (act, act, vec, vec, mat, vec, vec, mat, vec, vec, vec, mat, vec, mat, vec)
    return jax.shard_map(
        functools.partial(shards, mesh.shape["seq"]),
        mesh=mesh,
        in_specs=in_specs,
        out_specs=out_specs,
        check_vma=False,
    )
```

time: 1310 us -> 669 us (0.51)
  matrix products: 342 us -> 120 us
  local copies, waits for them, and re-layouts: 291 us -> 77.6 us
  waiting for transfers between devices: 367 us -> 172 us
  other arithmetic: 117 us -> 38.8 us
  Pallas kernels: 0 us -> 62.7 us
  starting transfers between devices: 33.7 us -> 60.1 us
  blocking collectives: 128 us -> 111 us
    dot_general x128 -> x14, matrix products: 342 us -> 120 us  [dot(): return lax.dot_general(a, b, dims, preferred_element_type=F32)]
    reduce_scatter x3 -> x4, waiting for transfers between devices: 210 us -> 24.5 us  [the longest x3 24.5 us: sum_owned(): lax.psum_scatter(grad.astype(BF16), 'fsdp', scatter_dimension=0, tiled=True)]
    while x157 -> x0, local copies, waits for them, and re-layouts: 90.5 us -> none
    all_to_all x8 -> x4, waiting for transfers between devices: 107 us -> 17.6 us  [the longest x2 10.5 us: shards(): moved = lax.all_to_all(sent, 'seq', split_axis=0, concat_axis=0, tiled=True)]
    psum x1, blocking collectives: 9.93 us -> 96.6 us  [shards(): late = lax.psum(first.astype(BF16), ('seq', 'fsdp')).astype(F32)]
    all_gather x9 -> x1, blocking collectives: 92 us -> 14.3 us  [shards(): vectors = lax.all_gather(packed, 'fsdp', axis=0, tiled=False)]
    ppermute x0 -> x33, waiting for transfers between devices: none -> 73.8 us  [swap(): return lax.ppermute(value, 'seq', [(i, i ^ r) for i in range(ring)])]
    pallas_call x0 -> x4, Pallas kernels: none -> 62.7 us  [the longest x2 38.6 us: attend_back(): pl.pallas_call(functools.partial(attend_back_kernel, bk=bk), grid_spec=pl...]
  transfers between devices with their start and end apart: 17 -> 45, of which waited for: 12 -> 17; matrix products, arithmetic and copies ran while one was open for 23% -> 28% of each run, Pallas kernels for 0% -> 6%
where the time goes in v1:
time: 669 us; the launch traced here: 658 us
  waiting for transfers between devices  172 us (26%)
  matrix products  120 us (18%)
  blocking collectives  111 us (17%)
  local copies, waits for them, and re-layouts  77.6 us (12%)
  Pallas kernels  62.7 us (9%)
  starting transfers between devices  60.1 us (9%)
  other arithmetic  38.8 us (6%)
  between operations  15.7 us (2%)
    dot_general x14, matrix products, dot(): return lax.dot_general(a, b, dims, preferred_element_type=F32)  120 us
    psum x1, blocking collectives, shards(): late = lax.psum(first.astype(BF16), ('seq', 'fsdp')).astype(F32)  96.6 us
    ppermute x33, waiting for transfers between devices, swap(): return lax.ppermute(value, 'seq', [(i, i ^ r) for i in range(ring)])  73.8 us
    all_gather x1, waiting for transfers between devices, shards(): w2 = lax.all_gather(w_fc2, 'fsdp', axis=0, tiled=True)  53.9 us
    ppermute x33, starting transfers between devices, swap(): return lax.ppermute(value, 'seq', [(i, i ^ r) for i in range(ring)])  43.7 us
    pallas_call x2, Pallas kernels, attend_back(): pl.pallas_call(functools.partial(attend_back_kernel, bk=bk), grid_spec=pl...  38.6 us
    dynamic_update_slice x18, local copies, waits for them, and re-layouts, gather_seq(): out = lax.dynamic_update_index_in_dim(out, swap(value, ring, r), me ^ r, 0)  28.9 us
    reduce_scatter x3, waiting for transfers between devices, sum_owned(): lax.psum_scatter(grad.astype(BF16), 'fsdp', scatter_dimension=0, tiled=True)  24.5 us
  transfers between devices with their start and end apart: 45, of which 17 were waited for; matrix products, arithmetic and copies ran while one was open for 28% of the time, Pallas kernels for 6%

profile of v1, /device:TPU:0, one launch (start us, length us, event | category | flops | bytes accessed | tf_op | source)
XLA Modules:
  0.0 658.0 jit_solution(13947807716376716694)
XLA Ops:
  22.9 14.3 %all-gather.1 = bf16[8,12,128]{2,1,0:T(8,128)(2,1)S(1)} all-gather(bf16[1,12,128]{2,1,0:T(8,128)(2,1)S(1)} %bitcast.286), channel_id=2, replica_groups=mesh['seq'=4,'fsdp'=8] {'fsdp'}, dimensions={0}, use_global_device_ids=true | all-gather | bytes 27648 | tf_op jit(solution)/shard_map/all_gather | solution.py:272
  42.3 13.8 %collective-permute-done.4 = bf16[392,1024]{1,0:T(8,128)(2,1)} collective-permute-done((bf16[392,1024]{1,0:T(8,128)(2,1)}, bf16[392,1024]{1,0:T(8,128)(2,1)}, u32[]{:S(2)}, u32[]{:S(2)}) %collective-permute-start.4) | collective-permute-done | bytes 802848 | tf_op jit(solution)/shard_map/ppermute | solution.py:198
  60.3 11.0 %collective-permute-done = bf16[392,1024]{1,0:T(8,128)(2,1)} collective-permute-done((bf16[392,1024]{1,0:T(8,128)(2,1)}, bf16[392,1024]{1,0:T(8,128)(2,1)}, u32[]{:S(2)}, u32[]{:S(2)}) %collective-permute-start) | collective-permute-done | bytes 802848 | tf_op jit(solution)/shard_map/ppermute | solution.py:198
  73.3 15.7 %collective-permute-done.1 = bf16[392,1024]{1,0:T(8,128)(2,1)} collective-permute-done((bf16[392,1024]{1,0:T(8,128)(2,1)}, bf16[392,1024]{1,0:T(8,128)(2,1)}, u32[]{:S(2)}, u32[]{:S(2)}) %collective-permute-start.1) | collective-permute-done | bytes 802848 | tf_op jit(solution)/shard_map/ppermute | solution.py:198
  98.9 5.6 add_convert_fusion
  104.5 5.1 fusion.12.q_ref.k_ref.v_ref
  109.6 13.5 %attend.2 = (bf16[1,1568,256]{2,1,0:T(8,128)(2,1)}, f32[1,4,1568]{2,1,0:T(4,128)S(1)}) custom-call(s32[1]{0:T(128)} %get-tuple-element.86.len_ref, bf16[1,1568,768]{2,1,0:T(8,128)(2,1)S(1)} %fusion.12.q_ref.k_ref.v_ref, bf16[1,1568,768]{2,1,0:T(8,128)(2,1)S(1)} %fusion.12.q_ref.k_ref.v_ref, bf16[1,1568,768]{2,1,0:T(8,128)(2,1)S(1)} %fusion.12.q_ref.k_ref.v_ref), custom_call_target="tpu_custom_call" | custom-call | flops 10070523904 | bytes 3211264 | tf_op jit(solution)/shard_map/attend/pallas_call | solution.py:146
  126.7 4.6 fusion.13.q_ref.k_ref.v_ref
  131.3 10.5 %attend.3 = (bf16[1,1568,256]{2,1,0:T(8,128)(2,1)}, f32[1,4,1568]{2,1,0:T(4,128)S(1)}) custom-call(s32[1]{0:T(128)} %get-tuple-element.85.len_ref, bf16[1,1568,768]{2,1,0:T(8,128)(2,1)S(1)} %fusion.13.q_ref.k_ref.v_ref, bf16[1,1568,768]{2,1,0:T(8,128)(2,1)S(1)} %fusion.13.q_ref.k_ref.v_ref, bf16[1,1568,768]{2,1,0:T(8,128)(2,1)S(1)} %fusion.13.q_ref.k_ref.v_ref), custom_call_target="tpu_custom_call" | custom-call | flops 10070523904 | bytes 3211264 | tf_op jit(solution)/shard_map/attend/pallas_call | solution.py:146
  143.3 4.6 all-to-all-start.1
  148.9 7.1 %all-to-all-done.1 = bf16[4,392,256]{2,1,0:T(8,128)(2,1)S(1)} async-done(((bf16[4,392,256]{2,1,0:T(8,128)(2,1)}), bf16[4,392,256]{2,1,0:T(8,128)(2,1)S(1)}, u32[]{:S(2)}, u32[]{:S(2)}) %all-to-all-start.1) | async-done | bytes 802848 | tf_op jit(solution)/shard_map/all_to_all | solution.py:292
  159.1 4.4 fusion.46
  165.7 15.7 %multiply_convert_fusion = (bf16[784,4096]{1,0:T(8,128)(2,1)}, f32[784,4096]{1,0:T(8,128)}) fusion(f32[4096]{0:T(1024)S(1)} %convert.60, bf16[1024,4096]{1,0:T(8,128)(2,1)} %all-gather.11.cloned.1.call-done, f32[784,1024]{1,0:T(8,128)} %copy-done.15, f32[1024]{0:T(1024)S(1)} %bitcast.288, f32[1024]{0:T(1024)S(1)} %bitcast.281, f32[784]{0:T(1024)S(1)} %add_rsqrt_fusion.3, ...), kind=kOutput, calls=%fused_computation.7 | convolution fusion | flops 6599950336 | bytes 30898304 | tf_op jit(solution)/shard_map/dot_general | solution.py:23
  181.3 53.9 %all-gather.13.cloned.1.call-done = bf16[4096,1024]{1,0:T(8,128)(2,1)} async-done(((bf16[512,1024]{1,0:T(8,128)(2,1)}), bf16[4096,1024]{1,0:T(8,128)(2,1)}) %all-gather.13.cloned.1.call-update) | async-done | bytes 8388624 | tf_op jit(solution)/shard_map/all_gather | solution.py:284
  235.2 16.7 %fusion.47 = (bf16[4096]{0:T(1024)(128)(2,1)S(1)}, bf16[784,4096]{1,0:T(8,128)(2,1)}) fusion(f32[784,4096]{1,0:T(8,128)} %get-tuple-element.90, f32[4096]{0:T(1024)S(1)} %convert.60, bf16[784,1024]{1,0:T(8,128)(2,1)S(1)} %bitcast.251, bf16[4096,1024]{1,0:T(8,128)(2,1)} %all-gather.13.cloned.1.call-done), kind=kOutput, calls=%fused_computation.165 | convolution fusion | flops 6615199744 | bytes 29286400 | tf_op jit(solution)/shard_map/dot_general | solution.py:23
  252.0 10.4 %multiply_reduce_fusion.4 = (bf16[1024]{0:T(1024)(128)(2,1)S(1)}, f32[784]{0:T(1024)S(1)}, f32[784]{0:T(1024)S(1)}, bf16[1024]{0:T(1024)(128)(2,1)S(1)}, f32[784,1024]{1,0:T(8,128)S(1)}) fusion(f32[784,1024]{1,0:T(8,128)S(1)} %copy-done.16, f32[784]{0:T(1024)S(1)} %add_rsqrt_fusion.3, f32[784]{0:T(1024)S(1)} %broadcast_multiply_fusion.7, ...), kind=kOutput, calls=%fused_computation.32 | convolution fusion | flops 6583889920 | bytes 21254400 | tf_op jit(solution)/shard_map/dot_general | solution.py:23
  271.6 10.5 %all-to-all-done.3 = bf16[4,392,256]{2,1,0:T(8,128)(2,1)S(1)} async-done(((bf16[4,392,256]{2,1,0:T(8,128)(2,1)}), bf16[4,392,256]{2,1,0:T(8,128)(2,1)S(1)}, u32[]{:S(2)}, u32[]{:S(2)}) %all-to-all-start.3) | async-done | bytes 802848 | tf_op jit(solution)/shard_map/all_to_all | solution.py:326
  288.1 16.6 %attend_back.3 = bf16[1,1568,768]{2,1,0:T(8,128)(2,1)S(1)} custom-call(s32[1]{0:T(128)} %get-tuple-element.85.len_ref, bf16[1,1568,768]{2,1,0:T(8,128)(2,1)S(1)} %copy-done.5, bf16[1,1568,768]{2,1,0:T(8,128)(2,1)S(1)} %copy-done.5, bf16[1,1568,768]{2,1,0:T(8,128)(2,1)S(1)} %copy-done.5, bf16[1,1568,256]{2,1,0:T(8,128)(2,1)S(1)} %bitcast.247, ...), custom_call_target="tpu_custom_call" | custom-call | flops 25176309760 | bytes 6422528 | tf_op jit(solution)/shard_map/attend_back/pallas_call | solution.py:176
  306.4 22.0 %attend_back.2 = bf16[1,1568,768]{2,1,0:T(8,128)(2,1)S(1)} custom-call(s32[1]{0:T(128)} %get-tuple-element.86.len_ref, bf16[1,1568,768]{2,1,0:T(8,128)(2,1)S(1)} %copy-done.3, bf16[1,1568,768]{2,1,0:T(8,128)(2,1)S(1)} %copy-done.3, bf16[1,1568,768]{2,1,0:T(8,128)(2,1)S(1)} %copy-done.3, bf16[1,1568,256]{2,1,0:T(8,128)(2,1)} %bitcast.44.do_ref, ...), custom_call_target="tpu_custom_call" | custom-call | flops 25176309760 | bytes 6422528 | tf_op jit(solution)/shard_map/attend_back/pallas_call | solution.py:176
  329.8 7.0 %fusion.14 = bf16[1024,768]{1,0:T(8,128)(2,1)} fusion(bf16[1568,768]{1,0:T(8,128)(2,1)S(1)} %bitcast.243, bf16[1568,768]{1,0:T(8,128)(2,1)S(1)} %bitcast.245, bf16[1568,1024]{1,0:T(8,128)(2,1)S(1)} %copy-done.18, bf16[1568,1024]{1,0:T(8,128)(2,1)S(1)} %copy-done.19), kind=kOutput, calls=%fused_computation.50 | convolution fusion | flops 4955766784 | bytes 12812288 | tf_op jit(solution)/shard_map/dot_general | solution.py:23
  336.9 6.1 convolution_convert_fusion.2
  343.0 14.6 %convolution_convert_fusion = bf16[1024,4096]{1,0:T(8,128)(2,1)} fusion(bf16[784,4096]{1,0:T(8,128)(2,1)} %get-tuple-element.95, f32[784,1024]{1,0:T(8,128)} %copy-done.15, f32[1024]{0:T(1024)S(1)} %bitcast.289, f32[1024]{0:T(1024)S(1)} %bitcast.284, f32[784]{0:T(1024)S(1)} %add_rsqrt_fusion.3, f32[784]{0:T(1024)S(1)} %broadcast_multiply_fusion.7), kind=kOutput, calls=%fused_computation.10 | convolution fusion | flops 6584877056 | bytes 18036864 | tf_op jit(solution)/shard_map/dot_general | solution.py:23
  357.9 14.3 %convolution_convert_fusion.1 = bf16[4096,1024]{1,0:T(8,128)(2,1)} fusion(bf16[784,4096]{1,0:T(8,128)(2,1)} %get-tuple-element.89, bf16[784,1024]{1,0:T(8,128)(2,1)} %bitcast.250), kind=kOutput, calls=%fused_computation.11 | convolution fusion | flops 6580862976 | bytes 16416768 | tf_op jit(solution)/shard_map/dot_general | solution.py:23
  378.1 12.7 %add_convert_fusion.4 = bf16[784,1024]{1,0:T(8,128)(2,1)} fusion(f32[784,1024]{1,0:T(8,128)} %copy-done.15, f32[1024]{0:T(1024)S(1)} %bitcast.287, bf16[784,4096]{1,0:T(8,128)(2,1)} %get-tuple-element.89, bf16[4096,1024]{1,0:T(8,128)(2,1)} %all-gather.13.cloned.1.call-done), kind=kOutput, calls=%fused_computation.38 | convolution fusion | flops 6579077120 | bytes 19632128 | tf_op jit(solution)/shard_map/dot_general | solution.py:23
  408.7 96.6 %all-reduce = (bf16[4,1024]{1,0:T(4,128)(2,1)S(1)}, bf16[8,1024]{1,0:T(8,128)(2,1)S(1)}) all-reduce(bf16[4,1024]{1,0:T(4,128)(2,1)S(1)} %pad_maximum_fusion.5, bf16[8,1024]{1,0:T(8,128)(2,1)S(1)} %concatenate.31), channel_id=1, replica_groups=mesh['seq'=4,'fsdp'=8] {'seq','fsdp'}, use_global_device_ids=true, to_apply=%region_17.18 | all-reduce | flops 12288 | bytes 49152 | tf_op jit(solution)/shard_map/psum | solution.py:368
  511.6 13.7 %collective-permute-done.6 = bf16[392,1024]{1,0:T(8,128)(2,1)S(1)} collective-permute-done((bf16[392,1024]{1,0:T(8,128)(2,1)}, bf16[392,1024]{1,0:T(8,128)(2,1)S(1)}, u32[]{:S(2)}, u32[]{:S(2)}) %collective-permute-start.6) | collective-permute-done | bytes 802848 | tf_op jit(solution)/shard_map/ppermute | solution.py:198
  541.0 4.7 multiply_add_fusion
  546.5 6.1 dynamic_update_slice.95
  557.2 6.1 dynamic_update_slice.96
  563.3 6.1 dynamic_update_slice.97
  569.4 6.1 dynamic_update_slice.98
  588.5 24.5 %reduce-scatter.11.cloned.1.call-done = bf16[512,1024]{1,0:T(8,128)(2,1)} async-done(((bf16[4096,1024]{1,0:T(8,128)(2,1)}), bf16[512,1024]{1,0:T(8,128)(2,1)}) %reduce-scatter.11.cloned.1.call-update) | async-done | bytes 1048592 | tf_op jit(solution)/shard_map/reduce_scatter | solution.py:218
  (303 shorter events, 167.6 us)
Async XLA Ops:
  7.2 97.3 %all-gather.7.cloned.1.call-start = ((), (), s32[]{:S(2)}) async-start(), calls=%async_computation.8 | async-start | bytes 1769472 | tf_op jit(solution)/shard_map/all_gather | solution.py:281
  9.5 149.6 %all-gather.9.cloned.1.call-start = ((), (), s32[]{:S(2)}) async-start(), calls=%async_computation.9 | async-start | bytes 2359296 | tf_op jit(solution)/shard_map/all_gather | solution.py:282
  10.2 155.4 %all-gather.11.cloned.1.call-start = ((), (), s32[]{:S(2)}) async-start(), calls=%async_computation.10 | async-start | bytes 9437184 | tf_op jit(solution)/shard_map/all_gather | solution.py:283
  11.0 224.3 %all-gather.13.cloned.1.call-start = ((), (), s32[]{:S(2)}) async-start(), calls=%async_computation.11 | async-start | bytes 9437184 | tf_op jit(solution)/shard_map/all_gather | solution.py:284
  14.8 25.1 %collective-permute-start.3 = (bf16[392,1024]{1,0:T(8,128)(2,1)}, bf16[392,1024]{1,0:T(8,128)(2,1)}, u32[]{:S(2)}, u32[]{:S(2)}) collective-permute-start(bf16[392,1024]{1,0:T(8,128)(2,1)} %get-tuple-element.53), channel_id=1, source_target_pairs={{0,8},{8,0},{16,24},{24,16},{1,9},{9,1},{17,25},{25,17},{2,10},{10... | collective-permute-start | bytes 2408456 | tf_op jit(solution)/shard_map/ppermute | solution.py:198
  17.8 38.3 %collective-permute-start.4 = (bf16[392,1024]{1,0:T(8,128)(2,1)}, bf16[392,1024]{1,0:T(8,128)(2,1)}, u32[]{:S(2)}, u32[]{:S(2)}) collective-permute-start(bf16[392,1024]{1,0:T(8,128)(2,1)} %get-tuple-element.53), channel_id=1, source_target_pairs={{0,16},{8,24},{16,0},{24,8},{1,17},{9,25},{17,1},{25,9},{2,18},{10... | collective-permute-start | bytes 2408456 | tf_op jit(solution)/shard_map/ppermute | solution.py:198
  19.3 38.0 %collective-permute-start.5 = (bf16[392,1024]{1,0:T(8,128)(2,1)}, bf16[392,1024]{1,0:T(8,128)(2,1)}, u32[]{:S(2)}, u32[]{:S(2)}) collective-permute-start(bf16[392,1024]{1,0:T(8,128)(2,1)} %get-tuple-element.53), channel_id=1, source_target_pairs={{0,24},{8,16},{16,8},{24,0},{1,25},{9,17},{17,9},{25,1},{2,26},{10... | collective-permute-start | bytes 2408456 | tf_op jit(solution)/shard_map/ppermute | solution.py:198
  19.3 52.0 %collective-permute-start = (bf16[392,1024]{1,0:T(8,128)(2,1)}, bf16[392,1024]{1,0:T(8,128)(2,1)}, u32[]{:S(2)}, u32[]{:S(2)}) collective-permute-start(bf16[392,1024]{1,0:T(8,128)(2,1)} %get-tuple-element.54), channel_id=1, source_target_pairs={{0,8},{8,0},{16,24},{24,16},{1,9},{9,1},{17,25},{25,17},{2,10},{10... | collective-permute-start | bytes 2408456 | tf_op jit(solution)/shard_map/ppermute | solution.py:198
  21.3 67.8 %collective-permute-start.1 = (bf16[392,1024]{1,0:T(8,128)(2,1)}, bf16[392,1024]{1,0:T(8,128)(2,1)}, u32[]{:S(2)}, u32[]{:S(2)}) collective-permute-start(bf16[392,1024]{1,0:T(8,128)(2,1)} %get-tuple-element.54), channel_id=1, source_target_pairs={{0,16},{8,24},{16,0},{24,8},{1,17},{9,25},{17,1},{25,9},{2,18},{10... | collective-permute-start | bytes 2408456 | tf_op jit(solution)/shard_map/ppermute | solution.py:198
  40.0 51.1 %collective-permute-start.2 = (bf16[392,1024]{1,0:T(8,128)(2,1)}, bf16[392,1024]{1,0:T(8,128)(2,1)}, u32[]{:S(2)}, u32[]{:S(2)}) collective-permute-start(bf16[392,1024]{1,0:T(8,128)(2,1)} %get-tuple-element.54), channel_id=1, source_target_pairs={{0,24},{8,16},{16,8},{24,0},{1,25},{9,17},{17,9},{25,1},{2,26},{10... | collective-permute-start | bytes 2408456 | tf_op jit(solution)/shard_map/ppermute | solution.py:198
  123.2 20.1 %all-to-all-start = ((bf16[4,392,256]{2,1,0:T(8,128)(2,1)}), bf16[4,392,256]{2,1,0:T(8,128)(2,1)S(1)}, u32[]{:S(2)}, u32[]{:S(2)}) async-start(bf16[4,392,256]{2,1,0:T(8,128)(2,1)} %bitcast.26), calls=%async_computation | async-start | bytes 1605632 | tf_op jit(solution)/shard_map/all_to_all | solution.py:292
  282.1 22.6 %all-to-all-start.2 = ((bf16[4,392,256]{2,1,0:T(8,128)(2,1)}), bf16[4,392,256]{2,1,0:T(8,128)(2,1)}, u32[]{:S(2)}, u32[]{:S(2)}) async-start(bf16[4,392,256]{2,1,0:T(8,128)(2,1)} %bitcast.241), calls=%async_computation.2 | async-start | bytes 1605632 | tf_op jit(solution)/shard_map/all_to_all | solution.py:326
  286.3 244.3 %reduce-scatter.5.cloned.1.call-start = ((), (), s32[]{:S(2)}) async-start(), calls=%async_computation.12 | async-start | bytes 1769472 | tf_op jit(solution)/shard_map/reduce_scatter | solution.py:339
  336.8 199.1 %reduce-scatter.7.cloned.1.call-start = ((), (), s32[]{:S(2)}) async-start(), calls=%async_computation.13 | async-start | bytes 2359296 | tf_op jit(solution)/shard_map/reduce_scatter | solution.py:218
  343.0 240.7 %reduce-scatter.9.cloned.1.call-start = ((), (), s32[]{:S(2)}) async-start(), calls=%async_computation.14 | async-start | bytes 9437184 | tf_op jit(solution)/shard_map/reduce_scatter | solution.py:218
  357.7 255.3 %reduce-scatter.11.cloned.1.call-start = ((), (), s32[]{:S(2)}) async-start(), calls=%async_computation.15 | async-start | bytes 9437184 | tf_op jit(solution)/shard_map/reduce_scatter | solution.py:218
  395.8 109.5 %collective-permute-start.11 = (bf16[392,1024]{1,0:T(8,128)(2,1)}, bf16[392,1024]{1,0:T(8,128)(2,1)S(1)}, u32[]{:S(2)}, u32[]{:S(2)}) collective-permute-start(bf16[392,1024]{1,0:T(8,128)(2,1)} %get-tuple-element.49), channel_id=1, source_target_pairs={{0,24},{8,16},{16,8},{24,0},{1,25},{9,17},{17,9},{25,1},{2,26},{10... | collective-permute-start | bytes 2408456 | tf_op jit(solution)/shard_map/ppermute | solution.py:198
  398.6 110.7 %collective-permute-start.10 = (bf16[392,1024]{1,0:T(8,128)(2,1)}, bf16[392,1024]{1,0:T(8,128)(2,1)}, u32[]{:S(2)}, u32[]{:S(2)}) collective-permute-start(bf16[392,1024]{1,0:T(8,128)(2,1)} %get-tuple-element.50), channel_id=1, source_target_pairs={{0,16},{8,24},{16,0},{24,8},{1,17},{9,25},{17,1},{25,9},{2,18},{10... | collective-permute-start | bytes 2408456 | tf_op jit(solution)/shard_map/ppermute | solution.py:198
  399.2 110.2 %collective-permute-start.9 = (bf16[392,1024]{1,0:T(8,128)(2,1)}, bf16[392,1024]{1,0:T(8,128)(2,1)}, u32[]{:S(2)}, u32[]{:S(2)}) collective-permute-start(bf16[392,1024]{1,0:T(8,128)(2,1)} %get-tuple-element.48), channel_id=1, source_target_pairs={{0,8},{8,0},{16,24},{24,16},{1,9},{9,1},{17,25},{25,17},{2,10},{10... | collective-permute-start | bytes 2408456 | tf_op jit(solution)/shard_map/ppermute | solution.py:198
  404.2 107.4 %collective-permute-start.8 = (bf16[392,1024]{1,0:T(8,128)(2,1)}, bf16[392,1024]{1,0:T(8,128)(2,1)}, u32[]{:S(2)}, u32[]{:S(2)}) collective-permute-start(bf16[392,1024]{1,0:T(8,128)(2,1)} %get-tuple-element.46), channel_id=1, source_target_pairs={{0,24},{8,16},{16,8},{24,0},{1,25},{9,17},{17,9},{25,1},{2,26},{10... | collective-permute-start | bytes 2408456 | tf_op jit(solution)/shard_map/ppermute | solution.py:198
  407.0 104.5 %collective-permute-start.7 = (bf16[392,1024]{1,0:T(8,128)(2,1)}, bf16[392,1024]{1,0:T(8,128)(2,1)}, u32[]{:S(2)}, u32[]{:S(2)}) collective-permute-start(bf16[392,1024]{1,0:T(8,128)(2,1)} %get-tuple-element.47), channel_id=1, source_target_pairs={{0,16},{8,24},{16,0},{24,8},{1,17},{9,25},{17,1},{25,9},{2,18},{10... | collective-permute-start | bytes 2408456 | tf_op jit(solution)/shard_map/ppermute | solution.py:198
  505.3 20.0 %collective-permute-start.6 = (bf16[392,1024]{1,0:T(8,128)(2,1)}, bf16[392,1024]{1,0:T(8,128)(2,1)S(1)}, u32[]{:S(2)}, u32[]{:S(2)}) collective-permute-start(bf16[392,1024]{1,0:T(8,128)(2,1)} %get-tuple-element.45), channel_id=1, source_target_pairs={{0,8},{8,0},{16,24},{24,16},{1,9},{9,1},{17,25},{25,17},{2,10},{10... | collective-permute-start | bytes 2408456 | tf_op jit(solution)/shard_map/ppermute | solution.py:198
  532.6 21.5 %collective-permute-start.13 = (bf16[128,3,256]{0,2,1:T(8,128)(2,1)S(1)}, bf16[128,3,256]{0,2,1:T(8,128)(2,1)}, u32[]{:S(2)}, u32[]{:S(2)}) collective-permute-start(bf16[128,3,256]{0,2,1:T(8,128)(2,1)S(1)} %bitcast.270), channel_id=1, source_target_pairs={{0,16},{8,24},{16,0},{24,8},{1,17},{9,25},{17,1},{25,9},{2,18},{10... | collective-permute-start | bytes 589832 | tf_op jit(solution)/shard_map/ppermute | solution.py:198
  534.3 21.3 %collective-permute-start.14 = (bf16[128,3,256]{0,2,1:T(8,128)(2,1)S(1)}, bf16[128,3,256]{0,2,1:T(8,128)(2,1)}, u32[]{:S(2)}, u32[]{:S(2)}) collective-permute-start(bf16[128,3,256]{0,2,1:T(8,128)(2,1)S(1)} %bitcast.271), channel_id=1, source_target_pairs={{0,24},{8,16},{16,8},{24,0},{1,25},{9,17},{17,9},{25,1},{2,26},{10... | collective-permute-start | bytes 589832 | tf_op jit(solution)/shard_map/ppermute | solution.py:198
  537.5 38.0 %collective-permute-start.17 = (bf16[32,1024]{1,0:T(8,128)(2,1)}, bf16[32,1024]{1,0:T(8,128)(2,1)S(1)}, u32[]{:S(2)}, u32[]{:S(2)}) collective-permute-start(bf16[32,1024]{1,0:T(8,128)(2,1)} %get-tuple-element.63), channel_id=1, source_target_pairs={{0,24},{8,16},{16,8},{24,0},{1,25},{9,17},{17,9},{25,1},{2,26},{10... | collective-permute-start | bytes 196616 | tf_op jit(solution)/shard_map/ppermute | solution.py:198
  538.8 36.7 %collective-permute-start.16 = (bf16[32,1024]{1,0:T(8,128)(2,1)}, bf16[32,1024]{1,0:T(8,128)(2,1)S(1)}, u32[]{:S(2)}, u32[]{:S(2)}) collective-permute-start(bf16[32,1024]{1,0:T(8,128)(2,1)} %get-tuple-element.64), channel_id=1, source_target_pairs={{0,16},{8,24},{16,0},{24,8},{1,17},{9,25},{17,1},{25,9},{2,18},{10... | collective-permute-start | bytes 196616 | tf_op jit(solution)/shard_map/ppermute | solution.py:198
  539.7 35.8 %collective-permute-start.15 = (bf16[32,1024]{1,0:T(8,128)(2,1)}, bf16[32,1024]{1,0:T(8,128)(2,1)}, u32[]{:S(2)}, u32[]{:S(2)}) collective-permute-start(bf16[32,1024]{1,0:T(8,128)(2,1)} %get-tuple-element.62), channel_id=1, source_target_pairs={{0,8},{8,0},{16,24},{24,16},{1,9},{9,1},{17,25},{25,17},{2,10},{10... | collective-permute-start | bytes 196616 | tf_op jit(solution)/shard_map/ppermute | solution.py:198
  584.9 32.2 %collective-permute-start.23 = (bf16[32,4096]{1,0:T(8,128)(2,1)S(1)}, bf16[32,4096]{1,0:T(8,128)(2,1)S(1)}, u32[]{:S(2)}, u32[]{:S(2)}) collective-permute-start(bf16[32,4096]{1,0:T(8,128)(2,1)S(1)} %get-tuple-element.60), channel_id=1, source_target_pairs={{0,24},{8,16},{16,8},{24,0},{1,25},{9,17},{17,9},{25,1},{2,26},{10... | collective-permute-start | bytes 786440 | tf_op jit(solution)/shard_map/ppermute | solution.py:198
  586.2 31.5 %collective-permute-start.22 = (bf16[32,4096]{1,0:T(8,128)(2,1)S(1)}, bf16[32,4096]{1,0:T(8,128)(2,1)S(1)}, u32[]{:S(2)}, u32[]{:S(2)}) collective-permute-start(bf16[32,4096]{1,0:T(8,128)(2,1)S(1)} %get-tuple-element.61), channel_id=1, source_target_pairs={{0,16},{8,24},{16,0},{24,8},{1,17},{9,25},{17,1},{25,9},{2,18},{10... | collective-permute-start | bytes 786440 | tf_op jit(solution)/shard_map/ppermute | solution.py:198
  587.7 30.0 %collective-permute-start.21 = (bf16[32,4096]{1,0:T(8,128)(2,1)S(1)}, bf16[32,4096]{1,0:T(8,128)(2,1)S(1)}, u32[]{:S(2)}, u32[]{:S(2)}) collective-permute-start(bf16[32,4096]{1,0:T(8,128)(2,1)S(1)} %get-tuple-element.59), channel_id=1, source_target_pairs={{0,8},{8,0},{16,24},{24,16},{1,9},{9,1},{17,25},{25,17},{2,10},{10... | collective-permute-start | bytes 786440 | tf_op jit(solution)/shard_map/ppermute | solution.py:198
  618.9 16.7 %collective-permute-start.24 = (bf16[32,4096]{1,0:T(8,128)(2,1)S(1)}, bf16[32,4096]{1,0:T(8,128)(2,1)S(1)}, u32[]{:S(2)}, u32[]{:S(2)}) collective-permute-start(bf16[32,4096]{1,0:T(8,128)(2,1)S(1)} %get-tuple-element.36), channel_id=1, source_target_pairs={{0,8},{8,0},{16,24},{24,16},{1,9},{9,1},{17,25},{25,17},{2,10},{10... | collective-permute-start | bytes 786440 | tf_op jit(solution)/shard_map/ppermute | solution.py:198
  624.3 17.0 %collective-permute-start.26 = (bf16[32,4096]{1,0:T(8,128)(2,1)S(1)}, bf16[32,4096]{1,0:T(8,128)(2,1)S(1)}, u32[]{:S(2)}, u32[]{:S(2)}) collective-permute-start(bf16[32,4096]{1,0:T(8,128)(2,1)S(1)} %get-tuple-element.36), channel_id=1, source_target_pairs={{0,24},{8,16},{16,8},{24,0},{1,25},{9,17},{17,9},{25,1},{2,26},{10... | collective-permute-start | bytes 786440 | tf_op jit(solution)/shard_map/ppermute | solution.py:198
  (60 other events, 804.3 us)
Sparse Core Ops, SparseCore 0:
  10.2 30.0 all-gather.6
  41.9 28.0 all-gather.8
  71.6 81.5 all-gather.10
  154.6 80.5 all-gather.12
  336.9 57.3 reduce-scatter.4
  397.0 33.8 reduce-scatter.6
  433.2 89.4 reduce-scatter.8
  525.0 87.9 reduce-scatter.10

commit v2 on v1

--- a/solution.py
+++ b/solution.py
@@ -214,11 +214,21 @@
     return total
 
 
-def sum_owned(grad, ring, me):
-    owned = lax.psum_scatter(grad.astype(BF16), "fsdp", scatter_dimension=0, tiled=True)
+def to_owners(grad):
+    return lax.psum_scatter(grad, "fsdp", scatter_dimension=0, tiled=True)
+
+
+def sum_owned(owned, ring, me):
     rows, width = owned.shape
     part = sum_seq(owned.reshape(ring, rows // ring, width), ring, me).astype(BF16)
     return gather_seq(part, ring, me).reshape(rows, width).astype(F32)
+
+
+def sum_vectors(rows, devices, ring):
+    count, width = rows.shape
+    sent = rows.reshape(count, devices, width // devices).transpose(1, 0, 2)
+    total = jnp.sum(lax.all_to_all(sent, "fsdp", split_axis=0, concat_axis=0, tiled=True), axis=0)
+    return total + sum(swap(total, ring, r) for r in range(1, ring))
 
 
 def normalize(values):
@@ -237,6 +247,7 @@
 
 def shards(
     ring,
+    devices,
     tokens,
     lengths,
     ln1_gain,
@@ -311,14 +322,16 @@
 
     dy = cotangent.reshape(total_rows, width)
     dy_f = dy.astype(F32)
-    grad_w2 = sum_owned(dot(hidden, dy, TN), ring, me)
+    term_w2 = dot(hidden, dy, TN).astype(BF16)
     dz = (dot(dy, w2, NT) * slope).astype(BF16)
-    grad_w1 = sum_owned(dot(h2, dz, TN), ring, me)
+    term_w1 = dot(h2, dz, TN).astype(BF16)
     dh2 = dot(dz, w1, NT)
     grad_middle = dy_f + normalize_back(dh2, n2, r2, g2)
     da = grad_middle.astype(BF16)
-    grad_wo = sum_owned(dot(attended, da, TN), ring, me)
+    term_wo = dot(attended, da, TN).astype(BF16)
     do = dot(da, wo, NT).astype(BF16)
+    do, term_w2, term_w1, term_wo = lax.optimization_barrier((do, term_w2, term_w1, term_wo))
+    owned_w2, owned_w1, owned_wo = (to_owners(t) for t in (term_w2, term_w1, term_wo))
 
     dqkv, own_terms, gain_sum, shift_sum = [], [], 0.0, 0.0
     for c in range(clips):
@@ -335,10 +348,16 @@
         own_terms.append(sum_seq(dh1.astype(BF16).reshape(ring, rows, width), ring, me))
         dqkv.append(d)
     dqkv = jnp.concatenate(dqkv, axis=0)
-    grad_mine = dot(jnp.concatenate(normed, axis=0), dqkv, TN)
-    owned = lax.psum_scatter(grad_mine.astype(BF16), "fsdp", scatter_dimension=0, tiled=True)
-    grad_qkv = gather_seq(owned.reshape(own, 3, local), ring, me)
-    grad_qkv = grad_qkv.transpose(1, 2, 0, 3).reshape(own, 3 * width).astype(F32)
+    grad_mine = dot(jnp.concatenate(normed, axis=0), dqkv, TN).astype(BF16)
+    grad_mine, owned_w2, owned_w1, owned_wo = lax.optimization_barrier(
+        (grad_mine, owned_w2, owned_w1, owned_wo)
+    )
+    owned = to_owners(grad_mine)
+    grad_w2, grad_w1, grad_wo = (sum_owned(o, ring, me) for o in (owned_w2, owned_w1, owned_wo))
+    grad_qkv = gather_seq(owned, ring, me).astype(F32)
+    grad_qkv = jnp.concatenate(
+        [grad_qkv[r, :, i * local : (i + 1) * local] for i in range(3) for r in range(ring)], axis=1
+    )
 
     bias_sum = jnp.sum(dqkv.astype(F32), axis=0)
     zeros = jnp.zeros((width,), F32)
@@ -358,15 +377,11 @@
             jnp.sum(da.astype(F32), axis=0),
         ]
     )
-    second = jnp.concatenate([second, jnp.sum(dz.astype(F32), axis=0).reshape(-1, width)])
-    at = lax.axis_index("fsdp") * own
-    small = lax.psum(second.astype(BF16), ("seq", "fsdp")).astype(F32)
-    four = lax.dynamic_slice_in_dim(small[:4], at, own, axis=1)
-    grad_c1 = lax.dynamic_slice_in_dim(
-        small[4:].reshape(-1), lax.axis_index("fsdp") * b_fc1.shape[0], b_fc1.shape[0]
-    )
-    late = lax.psum(first.astype(BF16), ("seq", "fsdp")).astype(F32)
-    late = lax.dynamic_slice_in_dim(late, at, own, axis=1)
+    c1_sum = jnp.sum(dz.astype(F32), axis=0).reshape(devices, -1, own).transpose(1, 0, 2)
+    second = jnp.concatenate([second, c1_sum.reshape(-1, width)])
+    four = sum_vectors(second, devices, ring)
+    grad_c1 = four[4:].reshape(-1)
+    late = sum_vectors(first, devices, ring)
 
     terms = jnp.concatenate(own_terms, axis=0)
     n1, r1 = normalize(inputs)
@@ -395,7 +410,7 @@
     in_specs = (act, vec, vec, vec, mat, vec, vec, mat, vec, vec, vec, mat, vec, mat, vec, act)
     out_specs = (act, act, vec, vec, mat, vec, vec, mat, vec, vec, vec, mat, vec, mat, vec)
     return jax.shard_map(
-        functools.partial(shards, mesh.shape["seq"]),
+        functools.partial(shards, mesh.shape["seq"], mesh.shape["fsdp"]),
         mesh=mesh,
         in_specs=in_specs,
         out_specs=out_specs,

time: 669 us -> 626 us (0.936)
  blocking collectives: 111 us -> 14.3 us
  waiting for transfers between devices: 172 us -> 218 us
  starting transfers between devices: 60.1 us -> 88.6 us
  local copies, waits for them, and re-layouts: 77.6 us -> 53.2 us
  other arithmetic: 38.8 us -> 31.5 us
  Pallas kernels: 62.7 us -> 69.9 us
    psum x1 -> x0, blocking collectives: 96.6 us -> none  [shards(): late = lax.psum(first.astype(BF16), ('seq', 'fsdp')).astype(F32)]
    ppermute x33 -> x39, waiting for transfers between devices: 73.8 us -> 140 us  [swap(): return lax.ppermute(value, 'seq', [(i, i ^ r) for i in range(ring)])]
    all_to_all x0 -> x2, starting transfers between devices: none -> 24 us  [sum_vectors(): lax.all_to_all(sent, 'fsdp', split_axis=0, concat_axis=0, tiled=True)]
    dynamic_update_slice x18, local copies, waits for them, and re-layouts: 28.9 us -> 7.37 us  [gather_seq(): out = lax.dynamic_update_index_in_dim(out, swap(value, ring, r), me ^ r, 0)]
    reduce_scatter x4, waiting for transfers between devices: 24.5 us -> 4.73 us  [to_owners(): return lax.psum_scatter(grad, 'fsdp', scatter_dimension=0, tiled=True)]
    all_to_all x2, waiting for transfers between devices: 10.5 us -> 0.01 us  [shards(): moved = lax.all_to_all(sent, 'seq', split_axis=0, concat_axis=0, tiled=True)]
    unnamed x98 -> x105, local copies, waits for them, and re-layouts: 14.5 us -> 22.3 us
    all_to_all x0 -> x2, waiting for transfers between devices: none -> 6.77 us  [sum_vectors(): lax.all_to_all(sent, 'fsdp', split_axis=0, concat_axis=0, tiled=True)]
  transfers between devices with their start and end apart: 45 -> 53, of which waited for: 17 -> 21; matrix products, arithmetic and copies ran while one was open for 28% -> 20% of each run, Pallas kernels for 6% -> 11%
where the time goes in v2:
time: 626 us; the launch traced here: 616 us
  waiting for transfers between devices  218 us (35%)
  matrix products  124 us (20%)
  starting transfers between devices  88.6 us (14%)
  Pallas kernels  69.9 us (11%)
  local copies, waits for them, and re-layouts  53.2 us (8%)
  other arithmetic  31.5 us (5%)
  between operations  15.7 us (3%)
  blocking collectives  14.3 us (2%)
    ppermute x39, waiting for transfers between devices, swap(): return lax.ppermute(value, 'seq', [(i, i ^ r) for i in range(ring)])  140 us
    dot_general x14, matrix products, dot(): return lax.dot_general(a, b, dims, preferred_element_type=F32)  124 us
    all_gather x1, waiting for transfers between devices, shards(): w2 = lax.all_gather(w_fc2, 'fsdp', axis=0, tiled=True)  57.3 us
    ppermute x39, starting transfers between devices, swap(): return lax.ppermute(value, 'seq', [(i, i ^ r) for i in range(ring)])  47.7 us
    pallas_call x2, Pallas kernels, attend_back(): pl.pallas_call(functools.partial(attend_back_kernel, bk=bk), grid_spec=pl...  43.2 us
    pallas_call x2, Pallas kernels, attend(): pl.pallas_call(functools.partial(attend_kernel, bk=bk), grid_spec=pltpu.P...  26.7 us
    all_to_all x2, starting transfers between devices, sum_vectors(): lax.all_to_all(sent, 'fsdp', split_axis=0, concat_axis=0, tiled=True)  24 us
    unnamed x105, local copies, waits for them, and re-layouts  22.3 us
  transfers between devices with their start and end apart: 53, of which 21 were waited for; matrix products, arithmetic and copies ran while one was open for 20% of the time, Pallas kernels for 11%

profile of v2, /device:TPU:0, one launch (start us, length us, event | category | flops | bytes accessed | tf_op | source)
XLA Modules:
  0.0 616.2 jit_solution(8416668715221425668)
XLA Ops:
  22.9 14.3 %all-gather.1 = bf16[8,12,128]{2,1,0:T(8,128)(2,1)S(1)} all-gather(bf16[1,12,128]{2,1,0:T(8,128)(2,1)S(1)} %bitcast.342), channel_id=2, replica_groups=mesh['seq'=4,'fsdp'=8] {'fsdp'}, dimensions={0}, use_global_device_ids=true | all-gather | bytes 27648 | tf_op jit(solution)/shard_map/all_gather | solution.py:283
  41.7 14.4 %collective-permute-done.1 = bf16[392,1024]{1,0:T(8,128)(2,1)} collective-permute-done((bf16[392,1024]{1,0:T(8,128)(2,1)}, bf16[392,1024]{1,0:T(8,128)(2,1)}, u32[]{:S(2)}, u32[]{:S(2)}) %collective-permute-start.1) | collective-permute-done | bytes 802848 | tf_op jit(solution)/shard_map/ppermute | solution.py:198
  61.4 9.8 %collective-permute-done.3 = bf16[392,1024]{1,0:T(8,128)(2,1)} collective-permute-done((bf16[392,1024]{1,0:T(8,128)(2,1)}, bf16[392,1024]{1,0:T(8,128)(2,1)}, u32[]{:S(2)}, u32[]{:S(2)}) %collective-permute-start.3) | collective-permute-done | bytes 802848 | tf_op jit(solution)/shard_map/ppermute | solution.py:198
  72.5 16.6 %collective-permute-done.4 = bf16[392,1024]{1,0:T(8,128)(2,1)} collective-permute-done((bf16[392,1024]{1,0:T(8,128)(2,1)}, bf16[392,1024]{1,0:T(8,128)(2,1)}, u32[]{:S(2)}, u32[]{:S(2)}) %collective-permute-start.4) | collective-permute-done | bytes 802848 | tf_op jit(solution)/shard_map/ppermute | solution.py:198
  93.3 5.7 add_convert_fusion
  99.0 5.1 fusion.12.q_ref.k_ref.v_ref
  104.1 10.9 %attend.2 = (bf16[1,1568,256]{2,1,0:T(8,128)(2,1)}, f32[1,4,1568]{2,1,0:T(4,128)S(1)}) custom-call(s32[1]{0:T(128)} %get-tuple-element.100.len_ref, bf16[1,1568,768]{2,1,0:T(8,128)(2,1)S(1)} %fusion.12.q_ref.k_ref.v_ref, bf16[1,1568,768]{2,1,0:T(8,128)(2,1)S(1)} %fusion.12.q_ref.k_ref.v_ref, bf16[1,1568,768]{2,1,0:T(8,128)(2,1)S(1)} %fusion.12.q_ref.k_ref.v_ref), custom_call_target="tpu_custom_call" | custom-call | flops 10070523904 | bytes 3211264 | tf_op jit(solution)/shard_map/attend/pallas_call | solution.py:146
  119.2 4.4 fusion.13.q_ref.k_ref.v_ref
  123.5 15.8 %attend.3 = (bf16[1,1568,256]{2,1,0:T(8,128)(2,1)}, f32[1,4,1568]{2,1,0:T(4,128)S(1)}) custom-call(s32[1]{0:T(128)} %get-tuple-element.99.len_ref, bf16[1,1568,768]{2,1,0:T(8,128)(2,1)S(1)} %fusion.13.q_ref.k_ref.v_ref, bf16[1,1568,768]{2,1,0:T(8,128)(2,1)S(1)} %fusion.13.q_ref.k_ref.v_ref, bf16[1,1568,768]{2,1,0:T(8,128)(2,1)S(1)} %fusion.13.q_ref.k_ref.v_ref), custom_call_target="tpu_custom_call" | custom-call | flops 10070523904 | bytes 3211264 | tf_op jit(solution)/shard_map/attend/pallas_call | solution.py:146
  146.3 6.7 %all-to-all-done.1 = bf16[4,392,256]{2,1,0:T(8,128)(2,1)S(1)} async-done(((bf16[4,392,256]{2,1,0:T(8,128)(2,1)}), bf16[4,392,256]{2,1,0:T(8,128)(2,1)S(1)}, u32[]{:S(2)}, u32[]{:S(2)}) %all-to-all-start.1) | async-done | bytes 802848 | tf_op jit(solution)/shard_map/all_to_all | solution.py:303
  161.3 16.7 %multiply_convert_fusion = (bf16[784,4096]{1,0:T(8,128)(2,1)}, f32[784,4096]{1,0:T(8,128)}) fusion(f32[4096]{0:T(1024)S(1)} %convert.12, bf16[1024,4096]{1,0:T(8,128)(2,1)} %all-gather.11.cloned.1.call-done, f32[784,1024]{1,0:T(8,128)} %copy-done.15, f32[1024]{0:T(1024)S(1)} %bitcast.349, f32[1024]{0:T(1024)S(1)} %bitcast.335, f32[784]{0:T(1024)S(1)} %add_rsqrt_fusion.3, ...), kind=kOutput, calls=%fused_computation.8 | convolution fusion | flops 6599950336 | bytes 30898304 | tf_op jit(solution)/shard_map/dot_general | solution.py:23
  178.0 57.3 %all-gather.13.cloned.1.call-done = bf16[4096,1024]{1,0:T(8,128)(2,1)} async-done(((bf16[512,1024]{1,0:T(8,128)(2,1)}), bf16[4096,1024]{1,0:T(8,128)(2,1)}) %all-gather.13.cloned.1.call-update) | async-done | bytes 8388624 | tf_op jit(solution)/shard_map/all_gather | solution.py:295
  235.2 14.1 %convert_reduce_fusion = (f32[4096]{0:T(1024)S(1)}, bf16[784,4096]{1,0:T(8,128)(2,1)S(1)}) fusion(f32[784,4096]{1,0:T(8,128)} %get-tuple-element.104, f32[4096]{0:T(1024)S(1)} %convert.12, bf16[784,1024]{1,0:T(8,128)(2,1)S(1)} %bitcast.310, bf16[4096,1024]{1,0:T(8,128)(2,1)} %all-gather.13.cloned.1.call-done), kind=kOutput, calls=%fused_computation.7 | convolution fusion | flops 6618411008 | bytes 29294592 | tf_op jit(solution)/shard_map/dot_general | solution.py:23
  252.1 11.8 %convolution_convert_fusion = bf16[1024,4096]{1,0:T(8,128)(2,1)} fusion(bf16[784,4096]{1,0:T(8,128)(2,1)S(1)} %get-tuple-element.109, f32[784,1024]{1,0:T(8,128)S(1)} %copy-done.16, f32[1024]{0:T(1024)S(1)} %bitcast.350, f32[1024]{0:T(1024)S(1)} %bitcast.336, f32[784]{0:T(1024)S(1)} %add_rsqrt_fusion.3, f32[784]{0:T(1024)S(1)} %broadcast_multiply_fusion.7), kind=kOutput, calls=%fused_computation.11 | convolution fusion | flops 6584877056 | bytes 18036864 | tf_op jit(solution)/shard_map/dot_general | solution.py:23
  263.9 13.1 %multiply_reduce_fusion.4 = (f32[1024]{0:T(1024)S(1)}, f32[784]{0:T(1024)S(1)}, f32[784]{0:T(1024)S(1)}, f32[1024]{0:T(1024)S(1)}, f32[784,1024]{1,0:T(8,128)S(1)}) fusion(f32[784,1024]{1,0:T(8,128)} %copy-done.15, f32[784]{0:T(1024)S(1)} %add_rsqrt_fusion.3, f32[784]{0:T(1024)S(1)} %broadcast_multiply_fusion.7, f32[1024]{0:T(1024)S(1)} %bitcast.337, ...), kind=kOutput, calls=%fused_computation.35 | convolution fusion | flops 6583889920 | bytes 21258496 | tf_op jit(solution)/shard_map/dot_general | solution.py:23
  280.1 5.2 convolution_convert_fusion.2
  285.3 14.1 %convolution_convert_fusion.1 = bf16[4096,1024]{1,0:T(8,128)(2,1)} fusion(bf16[784,4096]{1,0:T(8,128)(2,1)} %get-tuple-element.103, bf16[784,1024]{1,0:T(8,128)(2,1)S(1)} %bitcast.311), kind=kOutput, calls=%fused_computation.12 | convolution fusion | flops 6580862976 | bytes 16416768 | tf_op jit(solution)/shard_map/dot_general | solution.py:23
  299.4 5.6 convolution_convert_fusion.3
  325.2 12.5 %add_convert_fusion.4 = bf16[784,1024]{1,0:T(8,128)(2,1)} fusion(f32[784,1024]{1,0:T(8,128)} %copy-done.15, f32[1024]{0:T(1024)S(1)} %bitcast.348, bf16[784,4096]{1,0:T(8,128)(2,1)} %get-tuple-element.103, bf16[4096,1024]{1,0:T(8,128)(2,1)} %all-gather.13.cloned.1.call-done), kind=kOutput, calls=%fused_computation.41 | convolution fusion | flops 6579077120 | bytes 19632128 | tf_op jit(solution)/shard_map/dot_general | solution.py:23
  345.1 17.9 %attend_back.2 = bf16[1,1568,768]{2,1,0:T(8,128)(2,1)S(1)} custom-call(s32[1]{0:T(128)} %get-tuple-element.100.len_ref, bf16[1,1568,768]{2,1,0:T(8,128)(2,1)S(1)} %copy-done.5, bf16[1,1568,768]{2,1,0:T(8,128)(2,1)S(1)} %copy-done.5, bf16[1,1568,768]{2,1,0:T(8,128)(2,1)S(1)} %copy-done.5, bf16[1,1568,256]{2,1,0:T(8,128)(2,1)S(1)} %bitcast.307, ...), custom_call_target="tpu_custom_call" | custom-call | flops 25176309760 | bytes 6422528 | tf_op jit(solution)/shard_map/attend_back/pallas_call | solution.py:176
  373.3 25.4 %attend_back.3 = bf16[1,1568,768]{2,1,0:T(8,128)(2,1)S(1)} custom-call(s32[1]{0:T(128)} %get-tuple-element.99.len_ref, bf16[1,1568,768]{2,1,0:T(8,128)(2,1)S(1)} %copy-done.3, bf16[1,1568,768]{2,1,0:T(8,128)(2,1)S(1)} %copy-done.3, bf16[1,1568,768]{2,1,0:T(8,128)(2,1)S(1)} %copy-done.3, bf16[1,1568,256]{2,1,0:T(8,128)(2,1)} %bitcast.52.do_ref, ...), custom_call_target="tpu_custom_call" | custom-call | flops 25176309760 | bytes 6422528 | tf_op jit(solution)/shard_map/attend_back/pallas_call | solution.py:176
  402.0 4.5 multiply_reduce_fusion
  407.2 20.6 %all-to-all-start.4 = ((f32[8,4,128]{2,1,0:T(4,128)}), f32[8,4,128]{2,1,0:T(4,128)S(1)}, u32[]{:S(2)}, u32[]{:S(2)}) async-start(f32[8,4,128]{2,1,0:T(4,128)} %maximum_bitcast_fusion), calls=%async_computation.4 | async-start | bytes 32768 | tf_op jit(solution)/shard_map/all_to_all | solution.py:230
  442.3 23.7 %collective-permute-done.13 = f32[4,128]{1,0:T(4,128)S(1)} collective-permute-done((f32[4,128]{1,0:T(4,128)S(1)}, f32[4,128]{1,0:T(4,128)S(1)}, u32[]{:S(2)}, u32[]{:S(2)}) %collective-permute-start.13) | collective-permute-done | bytes 2080 | tf_op jit(solution)/shard_map/ppermute | solution.py:198
  469.5 9.8 %fusion.14 = bf16[1024,768]{1,0:T(8,128)(2,1)} fusion(bf16[1568,768]{1,0:T(8,128)(2,1)S(1)} %bitcast.306, bf16[1568,768]{1,0:T(8,128)(2,1)S(1)} %bitcast.304, bf16[1568,1024]{1,0:T(8,128)(2,1)} %get-tuple-element.87, bf16[1568,1024]{1,0:T(8,128)(2,1)} %get-tuple-element.88), kind=kOutput, calls=%fused_computation.53 | convolution fusion | flops 4955766784 | bytes 12812288 | tf_op jit(solution)/shard_map/dot_general | solution.py:23
  482.1 21.9 %collective-permute-done.10 = bf16[392,1024]{1,0:T(8,128)(2,1)} collective-permute-done((bf16[392,1024]{1,0:T(8,128)(2,1)}, bf16[392,1024]{1,0:T(8,128)(2,1)}, u32[]{:S(2)}, u32[]{:S(2)}) %collective-permute-start.10) | collective-permute-done | bytes 802848 | tf_op jit(solution)/shard_map/ppermute | solution.py:198
  511.2 4.6 multiply_add_fusion
  515.8 4.7 reduce-scatter.7.cloned.1.call-done
  538.4 12.4 %collective-permute-done.22 = bf16[32,1024]{1,0:T(8,128)(2,1)S(1)} collective-permute-done((bf16[32,1024]{1,0:T(8,128)(2,1)S(1)}, bf16[32,1024]{1,0:T(8,128)(2,1)S(1)}, u32[]{:S(2)}, u32[]{:S(2)}) %collective-permute-start.22) | collective-permute-done | bytes 65568 | tf_op jit(solution)/shard_map/ppermute | solution.py:198
  550.8 5.1 collective-permute-done.23
  561.7 11.9 %collective-permute-done.34 = bf16[128,1024]{1,0:T(8,128)(2,1)S(1)} collective-permute-done((bf16[128,1024]{1,0:T(8,128)(2,1)S(1)}, bf16[128,1024]{1,0:T(8,128)(2,1)S(1)}, u32[]{:S(2)}, u32[]{:S(2)}) %collective-permute-start.34) | collective-permute-done | bytes 262176 | tf_op jit(solution)/shard_map/ppermute | solution.py:198
  586.1 8.0 %collective-permute-done.31 = bf16[32,4096]{1,0:T(8,128)(2,1)S(1)} collective-permute-done((bf16[32,4096]{1,0:T(8,128)(2,1)S(1)}, bf16[32,4096]{1,0:T(8,128)(2,1)S(1)}, u32[]{:S(2)}, u32[]{:S(2)}) %collective-permute-start.31) | collective-permute-done | bytes 262176 | tf_op jit(solution)/shard_map/ppermute | solution.py:198
  (313 shorter events, 175.9 us)
Async XLA Ops:
  7.2 91.8 %all-gather.7.cloned.1.call-start = ((), (), s32[]{:S(2)}) async-start(), calls=%async_computation.10 | async-start | bytes 1769472 | tf_op jit(solution)/shard_map/all_gather | solution.py:292
  9.5 145.5 %all-gather.9.cloned.1.call-start = ((), (), s32[]{:S(2)}) async-start(), calls=%async_computation.11 | async-start | bytes 2359296 | tf_op jit(solution)/shard_map/all_gather | solution.py:293
  10.2 151.1 %all-gather.11.cloned.1.call-start = ((), (), s32[]{:S(2)}) async-start(), calls=%async_computation.12 | async-start | bytes 9437184 | tf_op jit(solution)/shard_map/all_gather | solution.py:294
  11.0 224.3 %all-gather.13.cloned.1.call-start = ((), (), s32[]{:S(2)}) async-start(), calls=%async_computation.13 | async-start | bytes 9437184 | tf_op jit(solution)/shard_map/all_gather | solution.py:295
  14.8 25.1 %collective-permute-start = (bf16[392,1024]{1,0:T(8,128)(2,1)}, bf16[392,1024]{1,0:T(8,128)(2,1)}, u32[]{:S(2)}, u32[]{:S(2)}) collective-permute-start(bf16[392,1024]{1,0:T(8,128)(2,1)} %get-tuple-element.68), channel_id=1, source_target_pairs={{0,8},{8,0},{16,24},{24,16},{1,9},{9,1},{17,25},{25,17},{2,10},{10... | collective-permute-start | bytes 2408456 | tf_op jit(solution)/shard_map/ppermute | solution.py:198
  17.8 38.3 %collective-permute-start.1 = (bf16[392,1024]{1,0:T(8,128)(2,1)}, bf16[392,1024]{1,0:T(8,128)(2,1)}, u32[]{:S(2)}, u32[]{:S(2)}) collective-permute-start(bf16[392,1024]{1,0:T(8,128)(2,1)} %get-tuple-element.68), channel_id=1, source_target_pairs={{0,16},{8,24},{16,0},{24,8},{1,17},{9,25},{17,1},{25,9},{2,18},{10... | collective-permute-start | bytes 2408456 | tf_op jit(solution)/shard_map/ppermute | solution.py:198
  19.3 38.0 %collective-permute-start.2 = (bf16[392,1024]{1,0:T(8,128)(2,1)}, bf16[392,1024]{1,0:T(8,128)(2,1)}, u32[]{:S(2)}, u32[]{:S(2)}) collective-permute-start(bf16[392,1024]{1,0:T(8,128)(2,1)} %get-tuple-element.68), channel_id=1, source_target_pairs={{0,24},{8,16},{16,8},{24,0},{1,25},{9,17},{17,9},{25,1},{2,26},{10... | collective-permute-start | bytes 2408456 | tf_op jit(solution)/shard_map/ppermute | solution.py:198
  19.3 52.0 %collective-permute-start.3 = (bf16[392,1024]{1,0:T(8,128)(2,1)}, bf16[392,1024]{1,0:T(8,128)(2,1)}, u32[]{:S(2)}, u32[]{:S(2)}) collective-permute-start(bf16[392,1024]{1,0:T(8,128)(2,1)} %get-tuple-element.67), channel_id=1, source_target_pairs={{0,8},{8,0},{16,24},{24,16},{1,9},{9,1},{17,25},{25,17},{2,10},{10... | collective-permute-start | bytes 2408456 | tf_op jit(solution)/shard_map/ppermute | solution.py:198
  21.3 67.8 %collective-permute-start.4 = (bf16[392,1024]{1,0:T(8,128)(2,1)}, bf16[392,1024]{1,0:T(8,128)(2,1)}, u32[]{:S(2)}, u32[]{:S(2)}) collective-permute-start(bf16[392,1024]{1,0:T(8,128)(2,1)} %get-tuple-element.67), channel_id=1, source_target_pairs={{0,16},{8,24},{16,0},{24,8},{1,17},{9,25},{17,1},{25,9},{2,18},{10... | collective-permute-start | bytes 2408456 | tf_op jit(solution)/shard_map/ppermute | solution.py:198
  40.0 50.3 %collective-permute-start.5 = (bf16[392,1024]{1,0:T(8,128)(2,1)}, bf16[392,1024]{1,0:T(8,128)(2,1)}, u32[]{:S(2)}, u32[]{:S(2)}) collective-permute-start(bf16[392,1024]{1,0:T(8,128)(2,1)} %get-tuple-element.67), channel_id=1, source_target_pairs={{0,24},{8,16},{16,8},{24,0},{1,25},{9,17},{17,9},{25,1},{2,26},{10... | collective-permute-start | bytes 2408456 | tf_op jit(solution)/shard_map/ppermute | solution.py:198
  114.9 25.8 %all-to-all-start = ((bf16[4,392,256]{2,1,0:T(8,128)(2,1)}), bf16[4,392,256]{2,1,0:T(8,128)(2,1)}, u32[]{:S(2)}, u32[]{:S(2)}) async-start(bf16[4,392,256]{2,1,0:T(8,128)(2,1)} %bitcast.26), calls=%async_computation | async-start | bytes 1605632 | tf_op jit(solution)/shard_map/all_to_all | solution.py:303
  144.9 370.9 %reduce-scatter.9.cloned.1.call-start = ((), (), s32[]{:S(2)}) async-start(), calls=%async_computation.16 | async-start | bytes 2359296 | tf_op jit(solution)/shard_map/reduce_scatter | solution.py:218
  305.0 210.8 %reduce-scatter.5.cloned.1.call-start = ((), (), s32[]{:S(2)}) async-start(), calls=%async_computation.14 | async-start | bytes 9437184 | tf_op jit(solution)/shard_map/reduce_scatter | solution.py:218
  305.6 215.0 %reduce-scatter.7.cloned.1.call-start = ((), (), s32[]{:S(2)}) async-start(), calls=%async_computation.15 | async-start | bytes 9437184 | tf_op jit(solution)/shard_map/reduce_scatter | solution.py:218
  317.7 21.5 %all-to-all-start.2 = ((bf16[4,392,256]{2,1,0:T(8,128)(2,1)}), bf16[4,392,256]{2,1,0:T(8,128)(2,1)S(1)}, u32[]{:S(2)}, u32[]{:S(2)}) async-start(bf16[4,392,256]{2,1,0:T(8,128)(2,1)} %bitcast.302), calls=%async_computation.2 | async-start | bytes 1605632 | tf_op jit(solution)/shard_map/all_to_all | solution.py:339
  339.2 32.5 %all-to-all-start.3 = ((bf16[4,392,256]{2,1,0:T(8,128)(2,1)}), bf16[4,392,256]{2,1,0:T(8,128)(2,1)}, u32[]{:S(2)}, u32[]{:S(2)}) async-start(bf16[4,392,256]{2,1,0:T(8,128)(2,1)} %bitcast.300), calls=%async_computation.3 | async-start | bytes 1605632 | tf_op jit(solution)/shard_map/all_to_all | solution.py:339
  369.7 98.2 %collective-permute-start.6 = (bf16[392,1024]{1,0:T(8,128)(2,1)}, bf16[392,1024]{1,0:T(8,128)(2,1)S(1)}, u32[]{:S(2)}, u32[]{:S(2)}) collective-permute-start(bf16[392,1024]{1,0:T(8,128)(2,1)} %get-tuple-element.59), channel_id=1, source_target_pairs={{0,8},{8,0},{16,24},{24,16},{1,9},{9,1},{17,25},{25,17},{2,10},{10... | collective-permute-start | bytes 2408456 | tf_op jit(solution)/shard_map/ppermute | solution.py:198
  407.2 26.3 %all-to-all-start.4 = ((f32[8,4,128]{2,1,0:T(4,128)}), f32[8,4,128]{2,1,0:T(4,128)S(1)}, u32[]{:S(2)}, u32[]{:S(2)}) async-start(f32[8,4,128]{2,1,0:T(4,128)} %maximum_bitcast_fusion), calls=%async_computation.4 | async-start | bytes 32768 | tf_op jit(solution)/shard_map/all_to_all | solution.py:230
  427.8 169.5 %reduce-scatter.11.cloned.1.call-start = ((), (), s32[]{:S(2)}) async-start(), calls=%async_computation.17 | async-start | bytes 1769472 | tf_op jit(solution)/shard_map/reduce_scatter | solution.py:218
  428.7 51.1 %collective-permute-start.7 = (bf16[392,1024]{1,0:T(8,128)(2,1)}, bf16[392,1024]{1,0:T(8,128)(2,1)}, u32[]{:S(2)}, u32[]{:S(2)}) collective-permute-start(bf16[392,1024]{1,0:T(8,128)(2,1)} %get-tuple-element.61), channel_id=1, source_target_pairs={{0,16},{8,24},{16,0},{24,8},{1,17},{9,25},{17,1},{25,9},{2,18},{10... | collective-permute-start | bytes 2408456 | tf_op jit(solution)/shard_map/ppermute | solution.py:198
  433.9 32.0 %collective-permute-start.13 = (f32[4,128]{1,0:T(4,128)S(1)}, f32[4,128]{1,0:T(4,128)S(1)}, u32[]{:S(2)}, u32[]{:S(2)}) collective-permute-start(f32[4,128]{1,0:T(4,128)S(1)} %reduce_sum.249), channel_id=1, source_target_pairs={{0,16},{8,24},{16,0},{24,8},{1,17},{9,25},{17,1},{25,9},{2,18},{10... | collective-permute-start | bytes 6152 | tf_op jit(solution)/shard_map/ppermute | solution.py:198
  435.6 31.8 %collective-permute-start.14 = (f32[4,128]{1,0:T(4,128)S(1)}, f32[4,128]{1,0:T(4,128)S(1)}, u32[]{:S(2)}, u32[]{:S(2)}) collective-permute-start(f32[4,128]{1,0:T(4,128)S(1)} %reduce_sum.249), channel_id=1, source_target_pairs={{0,24},{8,16},{16,8},{24,0},{1,25},{9,17},{17,9},{25,1},{2,26},{10... | collective-permute-start | bytes 6152 | tf_op jit(solution)/shard_map/ppermute | solution.py:198
  440.3 39.5 %collective-permute-start.8 = (bf16[392,1024]{1,0:T(8,128)(2,1)}, bf16[392,1024]{1,0:T(8,128)(2,1)}, u32[]{:S(2)}, u32[]{:S(2)}) collective-permute-start(bf16[392,1024]{1,0:T(8,128)(2,1)} %get-tuple-element.60), channel_id=1, source_target_pairs={{0,24},{8,16},{16,8},{24,0},{1,25},{9,17},{17,9},{25,1},{2,26},{10... | collective-permute-start | bytes 2408456 | tf_op jit(solution)/shard_map/ppermute | solution.py:198
  466.0 38.0 %collective-permute-start.10 = (bf16[392,1024]{1,0:T(8,128)(2,1)}, bf16[392,1024]{1,0:T(8,128)(2,1)}, u32[]{:S(2)}, u32[]{:S(2)}) collective-permute-start(bf16[392,1024]{1,0:T(8,128)(2,1)} %get-tuple-element.64), channel_id=1, source_target_pairs={{0,16},{8,24},{16,0},{24,8},{1,17},{9,25},{17,1},{25,9},{2,18},{10... | collective-permute-start | bytes 2408456 | tf_op jit(solution)/shard_map/ppermute | solution.py:198
  467.4 36.6 %collective-permute-start.11 = (bf16[392,1024]{1,0:T(8,128)(2,1)}, bf16[392,1024]{1,0:T(8,128)(2,1)}, u32[]{:S(2)}, u32[]{:S(2)}) collective-permute-start(bf16[392,1024]{1,0:T(8,128)(2,1)} %get-tuple-element.63), channel_id=1, source_target_pairs={{0,24},{8,16},{16,8},{24,0},{1,25},{9,17},{17,9},{25,1},{2,26},{10... | collective-permute-start | bytes 2408456 | tf_op jit(solution)/shard_map/ppermute | solution.py:198
  467.8 37.9 %collective-permute-start.9 = (bf16[392,1024]{1,0:T(8,128)(2,1)}, bf16[392,1024]{1,0:T(8,128)(2,1)}, u32[]{:S(2)}, u32[]{:S(2)}) collective-permute-start(bf16[392,1024]{1,0:T(8,128)(2,1)} %get-tuple-element.62), channel_id=1, source_target_pairs={{0,8},{8,0},{16,24},{24,16},{1,9},{9,1},{17,25},{25,17},{2,10},{10... | collective-permute-start | bytes 2408456 | tf_op jit(solution)/shard_map/ppermute | solution.py:198
  526.2 35.5 %collective-permute-start.33 = (bf16[128,1024]{1,0:T(8,128)(2,1)S(1)}, bf16[128,1024]{1,0:T(8,128)(2,1)S(1)}, u32[]{:S(2)}, u32[]{:S(2)}) collective-permute-start(bf16[128,1024]{1,0:T(8,128)(2,1)S(1)} %get-tuple-element.70), channel_id=1, source_target_pairs={{0,8},{8,0},{16,24},{24,16},{1,9},{9,1},{17,25},{25,17},{2,10},{10... | collective-permute-start | bytes 786440 | tf_op jit(solution)/shard_map/ppermute | solution.py:198
  533.1 22.9 %collective-permute-start.27 = (bf16[32,4096]{1,0:T(8,128)(2,1)S(1)}, bf16[32,4096]{1,0:T(8,128)(2,1)S(1)}, u32[]{:S(2)}, u32[]{:S(2)}) collective-permute-start(bf16[32,4096]{1,0:T(8,128)(2,1)S(1)} %get-tuple-element.73), channel_id=1, source_target_pairs={{0,8},{8,0},{16,24},{24,16},{1,9},{9,1},{17,25},{25,17},{2,10},{10... | collective-permute-start | bytes 786440 | tf_op jit(solution)/shard_map/ppermute | solution.py:198
  534.6 21.9 %collective-permute-start.28 = (bf16[32,4096]{1,0:T(8,128)(2,1)S(1)}, bf16[32,4096]{1,0:T(8,128)(2,1)S(1)}, u32[]{:S(2)}, u32[]{:S(2)}) collective-permute-start(bf16[32,4096]{1,0:T(8,128)(2,1)S(1)} %get-tuple-element.75), channel_id=1, source_target_pairs={{0,16},{8,24},{16,0},{24,8},{1,17},{9,25},{17,1},{25,9},{2,18},{10... | collective-permute-start | bytes 786440 | tf_op jit(solution)/shard_map/ppermute | solution.py:198
  535.1 21.4 %collective-permute-start.29 = (bf16[32,4096]{1,0:T(8,128)(2,1)S(1)}, bf16[32,4096]{1,0:T(8,128)(2,1)S(1)}, u32[]{:S(2)}, u32[]{:S(2)}) collective-permute-start(bf16[32,4096]{1,0:T(8,128)(2,1)S(1)} %get-tuple-element.74), channel_id=1, source_target_pairs={{0,24},{8,16},{16,8},{24,0},{1,25},{9,17},{17,9},{25,1},{2,26},{10... | collective-permute-start | bytes 786440 | tf_op jit(solution)/shard_map/ppermute | solution.py:198
  556.0 17.6 %collective-permute-start.34 = (bf16[128,1024]{1,0:T(8,128)(2,1)S(1)}, bf16[128,1024]{1,0:T(8,128)(2,1)S(1)}, u32[]{:S(2)}, u32[]{:S(2)}) collective-permute-start(bf16[128,1024]{1,0:T(8,128)(2,1)S(1)} %get-tuple-element.72), channel_id=1, source_target_pairs={{0,16},{8,24},{16,0},{24,8},{1,17},{9,25},{17,1},{25,9},{2,18},{10... | collective-permute-start | bytes 786440 | tf_op jit(solution)/shard_map/ppermute | solution.py:198
  557.7 20.7 %collective-permute-start.30 = (bf16[32,4096]{1,0:T(8,128)(2,1)S(1)}, bf16[32,4096]{1,0:T(8,128)(2,1)S(1)}, u32[]{:S(2)}, u32[]{:S(2)}) collective-permute-start(bf16[32,4096]{1,0:T(8,128)(2,1)S(1)} %get-tuple-element.50), channel_id=1, source_target_pairs={{0,8},{8,0},{16,24},{24,16},{1,9},{9,1},{17,25},{25,17},{2,10},{10... | collective-permute-start | bytes 786440 | tf_op jit(solution)/shard_map/ppermute | solution.py:198
  (67 other events, 800.0 us)
Sparse Core Ops, SparseCore 0:
  10.2 30.0 all-gather.6
  41.9 28.0 all-gather.8
  71.6 81.5 all-gather.10
  154.6 80.5 all-gather.12
  305.1 34.1 reduce-scatter.8
  341.5 88.7 reduce-scatter.4
  432.6 87.9 reduce-scatter.6
  536.8 31.4 reduce-scatter.10

commit v3 on v2

--- a/solution.py
+++ b/solution.py
@@ -194,16 +194,107 @@
     )(lengths, qkv, qkv, qkv, grads, outs, logs)
 
 
+def mlp_piece_kernel(
+    core_ref, h_ref, ht_ref, dy_ref, mine_ref, other_ref, c1_ref, *rest, first, nz
+):
+    if first:
+        y_ref, dh_ref, keep_ref, send_ref, sums_ref, hm_ref, hmt_ref, w1_ref, w2_ref, u_ref, dz_ref = rest
+        yin_ref = dhin_ref = None
+    else:
+        yin_ref, dhin_ref, y_ref, dh_ref, keep_ref, send_ref, sums_ref, hm_ref, hmt_ref, w1_ref, w2_ref, u_ref, dz_ref = rest
+    core = core_ref[0]
+    width = h_ref.shape[1]
+    rows = mine_ref.shape[2]
+    half = nz * rows
+    def at(i, p):
+        block = 2 * i + (core if p == 0 else 1 - core)
+        return pl.ds(pl.multiple_of(block * rows, rows), rows)
+    def put(i, p):
+        return pl.ds(p * half + i * rows, rows)
+    for i in range(nz):
+        for p in range(2):
+            hm_ref[:, put(i, p)] = h_ref[:, at(i, p)]
+            hmt_ref[put(i, p), :] = ht_ref[at(i, p), :]
+            src = (mine_ref, other_ref)[p]
+            w2_ref[pl.ds((2 * i + p) * rows, rows), :] = src[i, 1]
+            for j in range(nz):
+                for r in range(2):
+                    w1_ref[put(i, p), pl.ds((2 * j + r) * rows, rows)] = src[i, 0, :, at(j, r)]
+    for i in range(nz):
+        cols = pl.ds(2 * i * rows, 2 * rows)
+        bias = jnp.concatenate([c1_ref[:, at(i, p)] for p in range(2)], axis=1)
+        z = dot(hm_ref[...], w1_ref[:, cols]) + bias
+        phi = 0.5 * (1.0 + lax.erf(z * (2.0 ** -0.5)))
+        u_ref[:, cols] = (z * phi).astype(BF16)
+        slope = phi + z * (jnp.exp(z * z * -0.5) * 0.3989422804014327)
+        dz = (dot(dy_ref[...], w2_ref[cols, :], NT) * slope).astype(BF16)
+        dz_ref[:, cols] = dz
+        s = jnp.sum(dz.astype(F32), axis=0, keepdims=True)
+        for p in range(2):
+            sums_ref[:, at(i, p)] = s[:, p * rows:(p + 1) * rows]
+        g2 = dot(u_ref[:, cols], dy_ref[...], TN).astype(BF16)
+        keep_ref[i, 1] = g2[:rows]
+        send_ref[i, 1] = g2[rows:]
+        g1 = dot(hmt_ref[...], dz_ref[:, cols]).astype(BF16)
+        for p in range(2):
+            part = g1[:, p * rows:(p + 1) * rows]
+            keep_ref[:, 0, :, at(i, p)] = part[:half].reshape(nz, rows, rows)
+            send_ref[:, 0, :, at(i, p)] = part[half:].reshape(nz, rows, rows)
+    for n in range(width // 256):
+        cols = pl.ds(256 * n, 256)
+        y = dot(u_ref[...], w2_ref[:, cols])
+        y_ref[:, cols] = y if first else y + yin_ref[:, cols]
+    for n in range(width // 256):
+        d = dot(dz_ref[...], w1_ref[pl.ds(256 * n, 256), :], NT)
+        for q in range(256 // rows):
+            p, i = divmod((256 // rows) * n + q, nz)
+            v = d[:, q * rows:(q + 1) * rows]
+            dh_ref[:, at(i, p)] = v if first else v + dhin_ref[:, at(i, p)]
+
+
+def mlp_piece(core, h2, h2t, dy, mine, other, c1, acc):
+    nz = mine.shape[0]
+    t, width = h2.shape
+    first = acc is None
+    vm = pl.BlockSpec(memory_space=pltpu.VMEM)
+    ins = [core, h2, h2t, dy, mine, other, c1] + ([] if first else list(acc))
+    specs = [pl.BlockSpec(memory_space=pltpu.SMEM)] + [vm] * (len(ins) - 1)
+    wide = jax.ShapeDtypeStruct((t, width), F32)
+    return pl.pallas_call(
+        functools.partial(mlp_piece_kernel, first=first, nz=nz),
+        in_specs=specs,
+        out_specs=[vm] * 5,
+        out_shape=[wide, wide, jax.ShapeDtypeStruct(mine.shape, BF16), jax.ShapeDtypeStruct(mine.shape, BF16), jax.ShapeDtypeStruct(c1.shape, F32)],
+        scratch_shapes=[pltpu.VMEM((t, width), BF16), pltpu.VMEM((width, t), BF16)] + [pltpu.VMEM((width, width), BF16)] * 2 + [pltpu.VMEM((t, width), BF16)] * 2,
+        input_output_aliases={} if first else {7: 0, 8: 1},
+        compiler_params=pltpu.CompilerParams(vmem_limit_bytes=40 << 20),
+        cost_estimate=pl.CostEstimate(flops=12 * t * width * width, bytes_accessed=20 << 20, transcendentals=2 * t * width),
+        name="mlp_piece",
+    )(*ins)
+
+
 def swap(value, ring, r):
     return lax.ppermute(value, "seq", [(i, i ^ r) for i in range(ring)])
 
 
 def gather_seq(value, ring, me):
     out = jnp.zeros((ring,) + value.shape, value.dtype)
-    out = lax.dynamic_update_index_in_dim(out, value, me, 0)
-    for r in range(1, ring):
-        out = lax.dynamic_update_index_in_dim(out, swap(value, ring, r), me ^ r, 0)
+    cut = value.shape[0] // 16 * 8
+    for r, part in enumerate(partners(value, ring, cut)):
+        out = lax.dynamic_update_index_in_dim(out, part, me ^ r, 0)
     return out
+
+
+def twin(value, devices):
+    return lax.ppermute(value, "fsdp", [(i, i ^ 1) for i in range(devices)])
+
+
+def partners(value, ring, cut):
+    if ring != 4:
+        return [value] + [swap(value, ring, r) for r in range(1, ring)]
+    one, two = swap(value, ring, 1), swap(value, ring, 2)
+    far = [swap(two[:cut], ring, 1), swap(one[cut:], ring, 2)]
+    return [value, one, two, jnp.concatenate(far, axis=0)]
 
 
 def sum_seq(terms, ring, me):
@@ -291,8 +382,18 @@
     mine = lax.dynamic_index_in_dim(w_qkv.reshape(own, 3, ring, local), me, 2, keepdims=False)
     wqkv = lax.all_gather(mine.reshape(own, 3 * local), "fsdp", axis=0, tiled=True)
     wo = lax.all_gather(w_out, "fsdp", axis=0, tiled=True)
-    w1 = lax.all_gather(w_fc1, "fsdp", axis=0, tiled=True)
-    w2 = lax.all_gather(w_fc2, "fsdp", axis=0, tiled=True)
+    quarters = ring == 4 and w_fc1.shape[1] == ring * width and devices % 2 == 0
+    if quarters:
+        core = lax.axis_index("fsdp") % 2
+        same_core = [list(range(p, devices, 2)) for p in range(2)]
+        part1 = lax.dynamic_index_in_dim(w_fc1.reshape(own, devices, ring, own), me, 2)
+        part2 = lax.dynamic_index_in_dim(w_fc2.reshape(ring, own, width), me, 0)
+        part = jnp.concatenate([part1.reshape(1, own, width), part2], axis=0)
+        part = lax.all_gather(part, "fsdp", axis=0, axis_index_groups=same_core)
+        pieces = [(p, twin(p, devices)) for p in partners(part, ring, devices // 4)]
+    else:
+        w1 = lax.all_gather(w_fc1, "fsdp", axis=0, tiled=True)
+        w2 = lax.all_gather(w_fc2, "fsdp", axis=0, tiled=True)
 
     normed, qkv, heads_out, logs, attended = [], [], [], [], []
     for c in range(clips):
@@ -314,24 +415,48 @@
     middle = inputs + (dot(attended, wo) + bo)
     n2, r2 = normalize(middle)
     h2 = (n2 * g2 + b2).astype(BF16)
-    z = dot(h2, w1) + c1
-    phi = 0.5 * (1.0 + lax.erf(z * (2.0 ** -0.5)))
-    hidden = (z * phi).astype(BF16)
-    slope = phi + z * (jnp.exp(-0.5 * z * z) * 0.3989422804014327)
-    layer_out = (middle + (dot(hidden, w2) + c2)).astype(BF16).reshape(clips, rows, width)
-
     dy = cotangent.reshape(total_rows, width)
     dy_f = dy.astype(F32)
-    term_w2 = dot(hidden, dy, TN).astype(BF16)
-    dz = (dot(dy, w2, NT) * slope).astype(BF16)
-    term_w1 = dot(h2, dz, TN).astype(BF16)
-    dh2 = dot(dz, w1, NT)
+    if quarters:
+        h2t, acc = h2.T, None
+        terms, c1_sum = [None] * ring, jnp.zeros((ring, width), F32)
+        for r in (1, 2, 3, 0):
+            shift = lax.dynamic_index_in_dim(c1.reshape(devices, ring, own), me ^ r, 1)
+            y, dh2, keep, send, sums = mlp_piece(
+                core[None], h2, h2t, dy, *pieces[r], shift.reshape(1, width), acc
+            )
+            acc = (y, dh2)
+            terms[r] = keep.astype(F32) + twin(send, devices).astype(F32)
+            c1_sum = lax.dynamic_update_slice_in_dim(c1_sum, sums, me ^ r, 0)
+        total = terms[0]
+        for r in range(1, ring):
+            total = total + swap(terms[r].astype(BF16), ring, r).astype(F32)
+        mlp_terms = (total.astype(BF16),)
+    else:
+        z = dot(h2, w1) + c1
+        phi = 0.5 * (1.0 + lax.erf(z * (2.0 ** -0.5)))
+        hidden = (z * phi).astype(BF16)
+        slope = phi + z * (jnp.exp(-0.5 * z * z) * 0.3989422804014327)
+        y = dot(hidden, w2)
+        dz = (dot(dy, w2, NT) * slope).astype(BF16)
+        dh2 = dot(dz, w1, NT)
+        mlp_terms = (dot(hidden, dy, TN).astype(BF16), dot(h2, dz, TN).astype(BF16))
+        c1_sum = jnp.sum(dz.astype(F32), axis=0).reshape(devices, -1, own).transpose(1, 0, 2)
+    layer_out = (middle + (y + c2)).astype(BF16).reshape(clips, rows, width)
+
     grad_middle = dy_f + normalize_back(dh2, n2, r2, g2)
     da = grad_middle.astype(BF16)
     term_wo = dot(attended, da, TN).astype(BF16)
     do = dot(da, wo, NT).astype(BF16)
-    do, term_w2, term_w1, term_wo = lax.optimization_barrier((do, term_w2, term_w1, term_wo))
-    owned_w2, owned_w1, owned_wo = (to_owners(t) for t in (term_w2, term_w1, term_wo))
+    owned_wo = to_owners(term_wo)
+    if quarters:
+        owned_mlp = (
+            lax.psum_scatter(
+                mlp_terms[0], "fsdp", scatter_dimension=0, tiled=True, axis_index_groups=same_core
+            ),
+        )
+    else:
+        owned_mlp = tuple(to_owners(t) for t in mlp_terms)
 
     dqkv, own_terms, gain_sum, shift_sum = [], [], 0.0, 0.0
     for c in range(clips):
@@ -349,11 +474,16 @@
         dqkv.append(d)
     dqkv = jnp.concatenate(dqkv, axis=0)
     grad_mine = dot(jnp.concatenate(normed, axis=0), dqkv, TN).astype(BF16)
-    grad_mine, owned_w2, owned_w1, owned_wo = lax.optimization_barrier(
-        (grad_mine, owned_w2, owned_w1, owned_wo)
-    )
+    grad_mine, owned_mlp, owned_wo = lax.optimization_barrier((grad_mine, owned_mlp, owned_wo))
     owned = to_owners(grad_mine)
-    grad_w2, grad_w1, grad_wo = (sum_owned(o, ring, me) for o in (owned_w2, owned_w1, owned_wo))
+    grad_wo = sum_owned(owned_wo, ring, me)
+    if quarters:
+        both = gather_seq(owned_mlp[0][0], ring, me).astype(F32)
+        grad_w1 = both[:, 0].reshape(ring, own, devices, own).transpose(1, 2, 0, 3)
+        grad_w1 = grad_w1.reshape(own, ring * width)
+        grad_w2 = both[:, 1].reshape(ring * own, width)
+    else:
+        grad_w2, grad_w1 = (sum_owned(o, ring, me) for o in owned_mlp)
     grad_qkv = gather_seq(owned, ring, me).astype(F32)
     grad_qkv = jnp.concatenate(
         [grad_qkv[r, :, i * local : (i + 1) * local] for i in range(3) for r in range(ring)], axis=1
@@ -377,7 +507,6 @@
             jnp.sum(da.astype(F32), axis=0),
         ]
     )
-    c1_sum = jnp.sum(dz.astype(F32), axis=0).reshape(devices, -1, own).transpose(1, 0, 2)
     second = jnp.concatenate([second, c1_sum.reshape(-1, width)])
     four = sum_vectors(second, devices, ring)
     grad_c1 = four[4:].reshape(-1)

time: 626 us -> 682 us (1.089); the launches traced: 616 us -> 679 us
  Pallas kernels: 69.9 us -> 174 us
  matrix products: 124 us -> 45.3 us
  other arithmetic: 31.5 us -> 65.1 us
  local copies, waits for them, and re-layouts: 53.2 us -> 79.3 us
  waiting for transfers between devices: 218 us -> 204 us
  starting transfers between devices: 88.6 us -> 80.8 us
    dot_general x14 -> x8, matrix products: 124 us -> 45.3 us  [dot(): return lax.dot_general(a, b, dims, preferred_element_type=F32)]
    pallas_call x0 -> x4, Pallas kernels: none -> 76.5 us  [mlp_piece(): pl.pallas_call(functools.partial(mlp_piece_kernel, first=first, nz=nz), i...]
    all_gather x2 -> x1, waiting for transfers between devices: 57.3 us -> 0.02 us  [shards(): part = lax.all_gather(part, 'fsdp', axis=0, axis_index_groups=same_core)]
    ppermute x39 -> x41, waiting for transfers between devices: 140 us -> 170 us  [swap(): return lax.ppermute(value, 'seq', [(i, i ^ r) for i in range(ring)])]
    all_to_all x2, waiting for transfers between devices: 6.72 us -> 29.2 us  [shards(): lax.all_to_all(out.reshape(ring, rows, local), 'seq', split_axis=0, conca...]
    convert_element_type x0 -> x5, other arithmetic: none -> 19.5 us  [the longest x3 11.6 us: shards(): total = total + swap(terms[r].astype(BF16), ring, r).astype(F32)]
    pallas_call x2, Pallas kernels: 43.2 us -> 60.5 us  [attend_back(): pl.pallas_call(functools.partial(attend_back_kernel, bk=bk), grid_spec=pl...]
    slice x1 -> x12, local copies, waits for them, and re-layouts: 0.01 us -> 12.6 us  [the longest x10 8.15 us: partners(): far = [swap(two[:cut], ring, 1), swap(one[cut:], ring, 2)]]
  transfers between devices with their start and end apart: 53 -> 61, of which waited for: 21 -> 22; matrix products, arithmetic and copies ran while one was open for 20% -> 25% of each run, Pallas kernels for 11% -> 26%
where the time goes in v3:
time: 682 us; the launch traced here: 679 us
  waiting for transfers between devices  204 us (30%)
  Pallas kernels  174 us (26%)
  starting transfers between devices  80.8 us (12%)
  local copies, waits for them, and re-layouts  79.3 us (12%)
  other arithmetic  65.1 us (10%)
  matrix products  45.3 us (7%)
  between operations  15.7 us (2%)
  blocking collectives  14.9 us (2%)
    ppermute x41, waiting for transfers between devices, swap(): return lax.ppermute(value, 'seq', [(i, i ^ r) for i in range(ring)])  170 us
    pallas_call x4, Pallas kernels, mlp_piece(): pl.pallas_call(functools.partial(mlp_piece_kernel, first=first, nz=nz), i...  76.5 us
    pallas_call x2, Pallas kernels, attend_back(): pl.pallas_call(functools.partial(attend_back_kernel, bk=bk), grid_spec=pl...  60.5 us
    ppermute x41, starting transfers between devices, swap(): return lax.ppermute(value, 'seq', [(i, i ^ r) for i in range(ring)])  49.2 us
    dot_general x8, matrix products, dot(): return lax.dot_general(a, b, dims, preferred_element_type=F32)  45.3 us
    pallas_call x2, Pallas kernels, attend(): pl.pallas_call(functools.partial(attend_kernel, bk=bk), grid_spec=pltpu.P...  37.4 us
    all_to_all x2, waiting for transfers between devices, shards(): lax.all_to_all(out.reshape(ring, rows, local), 'seq', split_axis=0, conca...  29.2 us
    unnamed x145, local copies, waits for them, and re-layouts  28.6 us
  transfers between devices with their start and end apart: 61, of which 22 were waited for; matrix products, arithmetic and copies ran while one was open for 25% of the time, Pallas kernels for 26%

profile of v3, /device:TPU:0, one launch (start us, length us, event | category | flops | bytes accessed | tf_op | source)
XLA Modules:
  0.0 679.2 jit_solution(3447031021566710519)
XLA Ops:
  23.5 14.9 %all-gather.2 = bf16[8,12,128]{2,1,0:T(8,128)(2,1)S(1)} all-gather(bf16[1,12,128]{2,1,0:T(8,128)(2,1)S(1)} %bitcast.329), channel_id=2, replica_groups=mesh['seq'=4,'fsdp'=8] {'fsdp'}, dimensions={0}, use_global_device_ids=true | all-gather | bytes 27648 | tf_op jit(solution)/shard_map/all_gather | solution.py:374
  45.3 11.8 %collective-permute-done.4 = bf16[392,1024]{1,0:T(8,128)(2,1)S(1)} collective-permute-done((bf16[392,1024]{1,0:T(8,128)(2,1)}, bf16[392,1024]{1,0:T(8,128)(2,1)S(1)}, u32[]{:S(2)}, u32[]{:S(2)}) %collective-permute-start.4) | collective-permute-done | bytes 802848 | tf_op jit(solution)/shard_map/ppermute | solution.py:277
  66.7 6.3 collective-permute-done.6
  86.0 6.1 add_convert_fusion
  92.1 5.1 fusion.6.q_ref.k_ref.v_ref
  97.3 18.9 %attend.2 = (bf16[1,1568,256]{2,1,0:T(8,128)(2,1)}, f32[1,4,1568]{2,1,0:T(4,128)S(1)}) custom-call(s32[1]{0:T(128)} %get-tuple-element.157.len_ref, bf16[1,1568,768]{2,1,0:T(8,128)(2,1)S(1)} %fusion.6.q_ref.k_ref.v_ref, bf16[1,1568,768]{2,1,0:T(8,128)(2,1)S(1)} %fusion.6.q_ref.k_ref.v_ref, bf16[1,1568,768]{2,1,0:T(8,128)(2,1)S(1)} %fusion.6.q_ref.k_ref.v_ref), custom_call_target="tpu_custom_call" | custom-call | flops 10070523904 | bytes 3211264 | tf_op jit(solution)/shard_map/attend/pallas_call | solution.py:146
  123.1 4.6 fusion.7.q_ref.k_ref.v_ref
  127.7 18.6 %attend.3 = (bf16[1,1568,256]{2,1,0:T(8,128)(2,1)}, f32[1,4,1568]{2,1,0:T(4,128)S(1)}) custom-call(s32[1]{0:T(128)} %get-tuple-element.156.len_ref, bf16[1,1568,768]{2,1,0:T(8,128)(2,1)S(1)} %fusion.7.q_ref.k_ref.v_ref, bf16[1,1568,768]{2,1,0:T(8,128)(2,1)S(1)} %fusion.7.q_ref.k_ref.v_ref, bf16[1,1568,768]{2,1,0:T(8,128)(2,1)S(1)} %fusion.7.q_ref.k_ref.v_ref), custom_call_target="tpu_custom_call" | custom-call | flops 10070523904 | bytes 3211264 | tf_op jit(solution)/shard_map/attend/pallas_call | solution.py:146
  154.1 29.2 %all-to-all-done.1 = bf16[4,392,256]{2,1,0:T(8,128)(2,1)S(1)} async-done(((bf16[4,392,256]{2,1,0:T(8,128)(2,1)}), bf16[4,392,256]{2,1,0:T(8,128)(2,1)S(1)}, u32[]{:S(2)}, u32[]{:S(2)}) %all-to-all-start.1) | async-done | bytes 802848 | tf_op jit(solution)/shard_map/all_to_all | solution.py:404
  204.3 8.2 %collective-permute-done.10 = bf16[2,2,128,1024]{3,2,1,0:T(8,128)(2,1)} collective-permute-done((bf16[2,2,128,1024]{3,2,1,0:T(8,128)(2,1)}, bf16[2,2,128,1024]{3,2,1,0:T(8,128)(2,1)}, u32[]{:S(2)}, u32[]{:S(2)}) %collective-permute-start.10) | collective-permute-done | bytes 1048608 | tf_op jit(solution)/shard_map/ppermute | solution.py:277
  214.8 8.2 %collective-permute-done.12 = bf16[2,2,128,1024]{3,2,1,0:T(8,128)(2,1)} collective-permute-done((bf16[2,2,128,1024]{3,2,1,0:T(8,128)(2,1)}, bf16[2,2,128,1024]{3,2,1,0:T(8,128)(2,1)}, u32[]{:S(2)}, u32[]{:S(2)}) %collective-permute-start.12) | collective-permute-done | bytes 1048608 | tf_op jit(solution)/shard_map/ppermute | solution.py:277
  225.9 17.9 %mlp_piece.4 = (f32[784,1024]{1,0:T(8,128)}, f32[784,1024]{1,0:T(8,128)}, bf16[4,2,128,1024]{3,2,1,0:T(8,128)(2,1)S(1)}, bf16[4,2,128,1024]{3,2,1,0:T(8,128)(2,1)}, f32[1,1024]{1,0:T(1,128)S(1)}) custom-call(s32[1]{0:T(128)} %bitcast.37.core_ref, bf16[784,1024]{1,0:T(8,128)(2,1)S(1)} %add_convert_fusion.9.h_ref, bf16[1024,784]{1,0:T(8,128)(2,1)S(1)} %copy-done.13, ...), custom_call_target="tpu_custom_call" | custom-call | flops 9865003008 | bytes 20971520 | tf_op jit(solution)/shard_map/mlp_piece/pallas_call | solution.py:263
  245.6 19.6 %mlp_piece.5 = (f32[784,1024]{1,0:T(8,128)}, f32[784,1024]{1,0:T(8,128)}, bf16[4,2,128,1024]{3,2,1,0:T(8,128)(2,1)S(1)}, bf16[4,2,128,1024]{3,2,1,0:T(8,128)(2,1)}, f32[1,1024]{1,0:T(1,128)S(1)}) custom-call(s32[1]{0:T(128)} %bitcast.37.core_ref, bf16[784,1024]{1,0:T(8,128)(2,1)S(1)} %add_convert_fusion.9.h_ref, ...), custom_call_target="tpu_custom_call", output_to_operand_aliasing={{0}: (7, {}), {1}: (8, {})} | custom-call | flops 9865003008 | bytes 20971520 | tf_op jit(solution)/shard_map/mlp_piece/pallas_call | solution.py:263
  269.8 19.6 %mlp_piece.6 = (f32[784,1024]{1,0:T(8,128)}, f32[784,1024]{1,0:T(8,128)}, bf16[4,2,128,1024]{3,2,1,0:T(8,128)(2,1)S(1)}, bf16[4,2,128,1024]{3,2,1,0:T(8,128)(2,1)}, f32[1,1024]{1,0:T(1,128)S(1)}) custom-call(s32[1]{0:T(128)} %bitcast.37.core_ref, bf16[784,1024]{1,0:T(8,128)(2,1)S(1)} %copy-done.16, ...), custom_call_target="tpu_custom_call", output_to_operand_aliasing={{0}: (7, {}), {1}: (8, {})} | custom-call | flops 9865003008 | bytes 20971520 | tf_op jit(solution)/shard_map/mlp_piece/pallas_call | solution.py:263
  290.7 19.4 %mlp_piece.7 = (f32[784,1024]{1,0:T(8,128)}, f32[784,1024]{1,0:T(8,128)}, bf16[4,2,128,1024]{3,2,1,0:T(8,128)(2,1)S(1)}, bf16[4,2,128,1024]{3,2,1,0:T(8,128)(2,1)}, f32[1,1024]{1,0:T(1,128)S(1)}) custom-call(s32[1]{0:T(128)} %bitcast.37.core_ref, bf16[784,1024]{1,0:T(8,128)(2,1)S(1)} %copy-done.16, ...), custom_call_target="tpu_custom_call", output_to_operand_aliasing={{0}: (7, {}), {1}: (8, {})} | custom-call | flops 9865003008 | bytes 20971520 | tf_op jit(solution)/shard_map/mlp_piece/pallas_call | solution.py:263
  314.3 6.0 convert_reduce_fusion.3
  320.9 6.8 %all-to-all-start.5 = ((f32[8,8,128]{2,1,0:T(8,128)}), f32[8,8,128]{2,1,0:T(8,128)S(1)}, u32[]{:S(2)}, u32[]{:S(2)}) async-start(f32[8,8,128]{2,1,0:T(8,128)} %bitcast.112), calls=%async_computation.8 | async-start | bytes 65536 | tf_op jit(solution)/shard_map/all_to_all | solution.py:321
  340.6 5.6 convolution_convert_fusion
  357.5 30.3 %attend_back.2 = bf16[1,1568,768]{2,1,0:T(8,128)(2,1)S(1)} custom-call(s32[1]{0:T(128)} %get-tuple-element.157.len_ref, bf16[1,1568,768]{2,1,0:T(8,128)(2,1)S(1)} %copy-done.23, bf16[1,1568,768]{2,1,0:T(8,128)(2,1)S(1)} %copy-done.23, bf16[1,1568,768]{2,1,0:T(8,128)(2,1)S(1)} %copy-done.23, bf16[1,1568,256]{2,1,0:T(8,128)(2,1)S(1)} %bitcast.286, ...), custom_call_target="tpu_custom_call" | custom-call | flops 25176309760 | bytes 6422528 | tf_op jit(solution)/shard_map/attend_back/pallas_call | solution.py:176
  411.5 30.1 %attend_back.3 = bf16[1,1568,768]{2,1,0:T(8,128)(2,1)S(1)} custom-call(s32[1]{0:T(128)} %get-tuple-element.156.len_ref, bf16[1,1568,768]{2,1,0:T(8,128)(2,1)S(1)} %copy-done.21, bf16[1,1568,768]{2,1,0:T(8,128)(2,1)S(1)} %copy-done.21, bf16[1,1568,768]{2,1,0:T(8,128)(2,1)S(1)} %copy-done.21, bf16[1,1568,256]{2,1,0:T(8,128)(2,1)} %bitcast.61.do_ref, ...), custom_call_target="tpu_custom_call" | custom-call | flops 25176309760 | bytes 6422528 | tf_op jit(solution)/shard_map/attend_back/pallas_call | solution.py:176
  444.0 14.8 %collective-permute-done.27 = bf16[4,2,128,1024]{3,2,1,0:T(8,128)(2,1)} collective-permute-done((bf16[4,2,128,1024]{3,2,1,0:T(8,128)(2,1)}, bf16[4,2,128,1024]{3,2,1,0:T(8,128)(2,1)}, u32[]{:S(2)}, u32[]{:S(2)}) %collective-permute-start.27) | collective-permute-done | bytes 2097184 | tf_op jit(solution)/shard_map/ppermute | solution.py:277
  458.7 44.7 %collective-permute-done.31 = bf16[4,2,128,1024]{3,2,1,0:T(8,128)(2,1)} collective-permute-done((bf16[4,2,128,1024]{3,2,1,0:T(8,128)(2,1)}, bf16[4,2,128,1024]{3,2,1,0:T(8,128)(2,1)}, u32[]{:S(2)}, u32[]{:S(2)}) %collective-permute-start.31) | collective-permute-done | bytes 2097184 | tf_op jit(solution)/shard_map/ppermute | solution.py:277
  503.4 7.4 %add_convert_fusion.4 = bf16[4,2,128,1024]{3,2,1,0:T(8,128)(2,1)} fusion(bf16[4,2,128,1024]{3,2,1,0:T(8,128)(2,1)} %collective-permute-done.31, bf16[4,2,128,1024]{3,2,1,0:T(8,128)(2,1)} %collective-permute-done.29, bf16[4,2,128,1024]{3,2,1,0:T(8,128)(2,1)} %collective-permute-done.27, bf16[4,2,128,1024]{3,2,1,0:T(8,128)(2,1)} %collective-permute-done.25, ...), kind=kLoop, calls=%fused_computation.20 | loop fusion | flops 10485760 | bytes 12582912 | tf_op jit(solution)/shard_map/convert_element_type | solution.py:434
  510.8 7.9 %multiply_reduce_fusion = (f32[1024]{0:T(1024)S(1)}, f32[1024]{0:T(1024)S(1)}, bf16[1568,1024]{1,0:T(8,128)(2,1)}) fusion(bf16[4,392,1024]{2,1,0:T(8,128)(2,1)} %fusion.16, f32[1568]{0:T(1024)S(1)} %copy-done.48, f32[1568]{0:T(1024)S(1)} %copy-done.46, bf16[1024,768]{0,1:T(8,128)(2,1)} %all-gather.7.cloned.1.call-done, bf16[1,1568,768]{2,1,0:T(8,128)(2,1)} %copy-done.3), kind=kOutput, calls=%fused_computation.9 | convolution fusion | flops 2477488128 | bytes 10424576 | tf_op jit(solution)/shard_map/dot_general | solution.py:23
  519.4 8.2 %all-to-all-start.4 = ((f32[8,4,128]{2,1,0:T(4,128)}), f32[8,4,128]{2,1,0:T(4,128)S(1)}, u32[]{:S(2)}, u32[]{:S(2)}) async-start(f32[8,4,128]{2,1,0:T(4,128)} %maximum_bitcast_fusion.4), calls=%async_computation.4 | async-start | bytes 32768 | tf_op jit(solution)/shard_map/all_to_all | solution.py:321
  528.8 4.6 all-to-all-done.4
  541.5 24.6 %collective-permute-done.23 = f32[4,128]{1,0:T(4,128)S(1)} collective-permute-done((f32[4,128]{1,0:T(4,128)S(1)}, f32[4,128]{1,0:T(4,128)S(1)}, u32[]{:S(2)}, u32[]{:S(2)}) %collective-permute-start.23) | collective-permute-done | bytes 2080 | tf_op jit(solution)/shard_map/ppermute | solution.py:277
  569.7 9.7 %fusion.8 = bf16[1024,768]{1,0:T(8,128)(2,1)} fusion(bf16[1568,768]{1,0:T(8,128)(2,1)S(1)} %bitcast.285, bf16[1568,768]{1,0:T(8,128)(2,1)S(1)} %bitcast.283, bf16[1568,1024]{1,0:T(8,128)(2,1)} %get-tuple-element.144, bf16[1568,1024]{1,0:T(8,128)(2,1)} %get-tuple-element.145), kind=kOutput, calls=%fused_computation.45 | convolution fusion | flops 4955766784 | bytes 12812288 | tf_op jit(solution)/shard_map/dot_general | solution.py:23
  582.1 5.1 collective-permute-done.19
  587.3 17.1 %collective-permute-done.20 = bf16[392,1024]{1,0:T(8,128)(2,1)} collective-permute-done((bf16[392,1024]{1,0:T(8,128)(2,1)}, bf16[392,1024]{1,0:T(8,128)(2,1)}, u32[]{:S(2)}, u32[]{:S(2)}) %collective-permute-start.20) | collective-permute-done | bytes 802848 | tf_op jit(solution)/shard_map/ppermute | solution.py:277
  616.4 5.0 multiply_add_fusion
  627.4 9.3 %collective-permute-done.40 = bf16[32,1024]{1,0:T(8,128)(2,1)S(1)} collective-permute-done((bf16[32,1024]{1,0:T(8,128)(2,1)S(1)}, bf16[32,1024]{1,0:T(8,128)(2,1)S(1)}, u32[]{:S(2)}, u32[]{:S(2)}) %collective-permute-start.40) | collective-permute-done | bytes 65568 | tf_op jit(solution)/shard_map/ppermute | solution.py:277
  (391 shorter events, 217.9 us)
Async XLA Ops:
  7.2 84.9 %all-gather.7.cloned.1.call-start = ((), (), s32[]{:S(2)}) async-start(), calls=%async_computation.9 | async-start | bytes 1769472 | tf_op jit(solution)/shard_map/all_gather | solution.py:383
  9.6 110.1 %all-gather.11.cloned.1.call-start = ((), (), s32[]{:S(2)}) async-start(), calls=%async_computation.14 | async-start | bytes 2621440 | tf_op jit(solution)/shard_map/all_gather | solution.py:392
  14.3 175.3 %all-gather.9.cloned.1.call-start = ((), (), s32[]{:S(2)}) async-start(), calls=%async_computation.10 | async-start | bytes 2359296 | tf_op jit(solution)/shard_map/all_gather | solution.py:384
  22.4 34.6 %collective-permute-start.4 = (bf16[392,1024]{1,0:T(8,128)(2,1)}, bf16[392,1024]{1,0:T(8,128)(2,1)S(1)}, u32[]{:S(2)}, u32[]{:S(2)}) collective-permute-start(bf16[392,1024]{1,0:T(8,128)(2,1)} %get-tuple-element.126), channel_id=1, source_target_pairs={{0,8},{8,0},{16,24},{24,16},{1,9},{9,1},{17,25},{25,17},{2,10},{10... | collective-permute-start | bytes 2408456 | tf_op jit(solution)/shard_map/ppermute | solution.py:277
  23.0 36.3 %collective-permute-start.5 = (bf16[392,1024]{1,0:T(8,128)(2,1)}, bf16[392,1024]{1,0:T(8,128)(2,1)}, u32[]{:S(2)}, u32[]{:S(2)}) collective-permute-start(bf16[392,1024]{1,0:T(8,128)(2,1)} %get-tuple-element.126), channel_id=1, source_target_pairs={{0,16},{8,24},{16,0},{24,8},{1,17},{9,25},{17,1},{25,9},{2,18},{10... | collective-permute-start | bytes 2408456 | tf_op jit(solution)/shard_map/ppermute | solution.py:277
  40.2 41.7 %collective-permute-start.3 = (bf16[200,1024]{1,0:T(8,128)(2,1)S(1)}, bf16[200,1024]{1,0:T(8,128)(2,1)S(1)}, u32[]{:S(2)}, u32[]{:S(2)}) collective-permute-start(bf16[200,1024]{1,0:T(8,128)(2,1)S(1)} %slice.211), channel_id=1, source_target_pairs={{0,16},{8,24},{16,0},{24,8},{1,17},{9,25},{17,1},{25,9},{2,18},{10... | collective-permute-start | bytes 1228808 | tf_op jit(solution)/shard_map/ppermute | solution.py:277
  43.8 38.0 %collective-permute-start.2 = (bf16[192,1024]{1,0:T(8,128)(2,1)}, bf16[192,1024]{1,0:T(8,128)(2,1)}, u32[]{:S(2)}, u32[]{:S(2)}) collective-permute-start(bf16[192,1024]{1,0:T(8,128)(2,1)} %slice.210), channel_id=1, source_target_pairs={{0,8},{8,0},{16,24},{24,16},{1,9},{9,1},{17,25},{25,17},{2,10},{10... | collective-permute-start | bytes 1179656 | tf_op jit(solution)/shard_map/ppermute | solution.py:277
  116.1 31.7 %all-to-all-start = ((bf16[4,392,256]{2,1,0:T(8,128)(2,1)}), bf16[4,392,256]{2,1,0:T(8,128)(2,1)S(1)}, u32[]{:S(2)}, u32[]{:S(2)}) async-start(bf16[4,392,256]{2,1,0:T(8,128)(2,1)} %bitcast.26), calls=%async_computation | async-start | bytes 1605632 | tf_op jit(solution)/shard_map/all_to_all | solution.py:404
  119.7 69.9 %collective-permute-start.11 = (bf16[4,2,128,1024]{3,2,1,0:T(8,128)(2,1)}, bf16[4,2,128,1024]{3,2,1,0:T(8,128)(2,1)}, u32[]{:S(2)}, u32[]{:S(2)}) collective-permute-start(bf16[4,2,128,1024]{3,2,1,0:T(8,128)(2,1)} %bitcast.287), channel_id=1, source_target_pairs={{0,8},{8,0},{16,24},{24,16},{1,9},{9,1},{17,25},{25,17},{2,10},{10... | collective-permute-start | bytes 6291464 | tf_op jit(solution)/shard_map/ppermute | solution.py:277
  121.6 64.2 %collective-permute-start.9 = (bf16[4,2,128,1024]{3,2,1,0:T(8,128)(2,1)}, bf16[4,2,128,1024]{3,2,1,0:T(8,128)(2,1)}, u32[]{:S(2)}, u32[]{:S(2)}) collective-permute-start(bf16[4,2,128,1024]{3,2,1,0:T(8,128)(2,1)} %bitcast.288), channel_id=1, source_target_pairs={{0,16},{8,24},{16,0},{24,8},{1,17},{9,25},{17,1},{25,9},{2,18},{10... | collective-permute-start | bytes 6291464 | tf_op jit(solution)/shard_map/ppermute | solution.py:277
  147.8 35.5 %all-to-all-start.1 = ((bf16[4,392,256]{2,1,0:T(8,128)(2,1)}), bf16[4,392,256]{2,1,0:T(8,128)(2,1)S(1)}, u32[]{:S(2)}, u32[]{:S(2)}) async-start(bf16[4,392,256]{2,1,0:T(8,128)(2,1)} %bitcast.34), calls=%async_computation.1 | async-start | bytes 1605632 | tf_op jit(solution)/shard_map/all_to_all | solution.py:404
  153.0 137.7 %collective-permute-start.8 = (bf16[4,2,128,1024]{3,2,1,0:T(8,128)(2,1)}, bf16[4,2,128,1024]{3,2,1,0:T(8,128)(2,1)}, u32[]{:S(2)}, u32[]{:S(2)}) collective-permute-start(bf16[4,2,128,1024]{3,2,1,0:T(8,128)(2,1)} %bitcast.289), channel_id=1, source_target_pairs={{0,1},{1,0},{2,3},{3,2},{4,5},{5,4},{6,7},{7,6},{8,9},{9,8},{10,11... | collective-permute-start | bytes 6291464 | tf_op jit(solution)/shard_map/ppermute | solution.py:289
  189.6 36.3 %collective-permute-start.15 = (bf16[4,2,128,1024]{3,2,1,0:T(8,128)(2,1)}, bf16[4,2,128,1024]{3,2,1,0:T(8,128)(2,1)}, u32[]{:S(2)}, u32[]{:S(2)}) collective-permute-start(bf16[4,2,128,1024]{3,2,1,0:T(8,128)(2,1)} %collective-permute-done.11.mine_ref), channel_id=1, source_target_pairs={{0,1},{1,0},{2,3},{3,2},{4,5},{5,4},{6,7},{7,6},{8,9},{9,8},{10,11... | collective-permute-start | bytes 6291464 | tf_op jit(solution)/shard_map/ppermute | solution.py:289
  198.1 47.5 %collective-permute-start.14 = (bf16[4,2,128,1024]{3,2,1,0:T(8,128)(2,1)}, bf16[4,2,128,1024]{3,2,1,0:T(8,128)(2,1)}, u32[]{:S(2)}, u32[]{:S(2)}) collective-permute-start(bf16[4,2,128,1024]{3,2,1,0:T(8,128)(2,1)} %collective-permute-done.9.mine_ref), channel_id=1, source_target_pairs={{0,1},{1,0},{2,3},{3,2},{4,5},{5,4},{6,7},{7,6},{8,9},{9,8},{10,11... | collective-permute-start | bytes 6291464 | tf_op jit(solution)/shard_map/ppermute | solution.py:289
  225.3 41.6 %collective-permute-start.13 = (bf16[4,2,128,1024]{3,2,1,0:T(8,128)(2,1)}, bf16[4,2,128,1024]{3,2,1,0:T(8,128)(2,1)}, u32[]{:S(2)}, u32[]{:S(2)}) collective-permute-start(bf16[4,2,128,1024]{3,2,1,0:T(8,128)(2,1)} %constant_dynamic-update-slice_fusion.2.mine_ref), channel_id=1, source_target_pairs={{0,1},{1,0},{2,3},{3,2},{4,5},{5,4},{6,7},{7,6},{8,9},{9,8},{10,11... | collective-permute-start | bytes 6291464 | tf_op jit(solution)/shard_map/ppermute | solution.py:289
  245.1 149.5 %collective-permute-start.26 = (bf16[4,2,128,1024]{3,2,1,0:T(8,128)(2,1)}, bf16[4,2,128,1024]{3,2,1,0:T(8,128)(2,1)}, u32[]{:S(2)}, u32[]{:S(2)}) collective-permute-start(bf16[4,2,128,1024]{3,2,1,0:T(8,128)(2,1)} %get-tuple-element.57), channel_id=1, source_target_pairs={{0,1},{1,0},{2,3},{3,2},{4,5},{5,4},{6,7},{7,6},{8,9},{9,8},{10,11... | collective-permute-start | bytes 6291464 | tf_op jit(solution)/shard_map/ppermute | solution.py:289
  266.5 133.7 %collective-permute-start.28 = (bf16[4,2,128,1024]{3,2,1,0:T(8,128)(2,1)}, bf16[4,2,128,1024]{3,2,1,0:T(8,128)(2,1)}, u32[]{:S(2)}, u32[]{:S(2)}) collective-permute-start(bf16[4,2,128,1024]{3,2,1,0:T(8,128)(2,1)} %get-tuple-element.59), channel_id=1, source_target_pairs={{0,1},{1,0},{2,3},{3,2},{4,5},{5,4},{6,7},{7,6},{8,9},{9,8},{10,11... | collective-permute-start | bytes 6291464 | tf_op jit(solution)/shard_map/ppermute | solution.py:289
  337.0 273.0 %reduce-scatter.6.cloned.1.call-start = ((), (), s32[]{:S(2)}) async-start(), calls=%async_computation.12 | async-start | bytes 2359296 | tf_op jit(solution)/shard_map/reduce_scatter | solution.py:309
  348.9 56.7 %collective-permute-start.30 = (bf16[4,2,128,1024]{3,2,1,0:T(8,128)(2,1)}, bf16[4,2,128,1024]{3,2,1,0:T(8,128)(2,1)}, u32[]{:S(2)}, u32[]{:S(2)}) collective-permute-start(bf16[4,2,128,1024]{3,2,1,0:T(8,128)(2,1)} %get-tuple-element.61), channel_id=1, source_target_pairs={{0,1},{1,0},{2,3},{3,2},{4,5},{5,4},{6,7},{7,6},{8,9},{9,8},{10,11... | collective-permute-start | bytes 6291464 | tf_op jit(solution)/shard_map/ppermute | solution.py:289
  348.9 95.1 %collective-permute-start.25 = (bf16[4,2,128,1024]{3,2,1,0:T(8,128)(2,1)}, bf16[4,2,128,1024]{3,2,1,0:T(8,128)(2,1)}, u32[]{:S(2)}, u32[]{:S(2)}) collective-permute-start(bf16[4,2,128,1024]{3,2,1,0:T(8,128)(2,1)} %get-tuple-element.55), channel_id=1, source_target_pairs={{0,1},{1,0},{2,3},{3,2},{4,5},{5,4},{6,7},{7,6},{8,9},{9,8},{10,11... | collective-permute-start | bytes 6291464 | tf_op jit(solution)/shard_map/ppermute | solution.py:289
  350.4 59.4 %all-to-all-start.3 = ((bf16[4,392,256]{2,1,0:T(8,128)(2,1)}), bf16[4,392,256]{2,1,0:T(8,128)(2,1)}, u32[]{:S(2)}, u32[]{:S(2)}) async-start(bf16[4,392,256]{2,1,0:T(8,128)(2,1)} %bitcast.274), calls=%async_computation.3 | async-start | bytes 1605632 | tf_op jit(solution)/shard_map/all_to_all | solution.py:464
  354.6 255.4 %reduce-scatter.4.cloned.1.call-start = ((), (), s32[]{:S(2)}) async-start(), calls=%async_computation.11 | async-start | bytes 2621440 | tf_op jit(solution)/shard_map/reduce_scatter | solution.py:454
  392.6 175.5 %collective-permute-start.16 = (bf16[392,1024]{1,0:T(8,128)(2,1)}, bf16[392,1024]{1,0:T(8,128)(2,1)}, u32[]{:S(2)}, u32[]{:S(2)}) collective-permute-start(bf16[392,1024]{1,0:T(8,128)(2,1)} %get-tuple-element.115), channel_id=1, source_target_pairs={{0,8},{8,0},{16,24},{24,16},{1,9},{9,1},{17,25},{25,17},{2,10},{10... | collective-permute-start | bytes 2408456 | tf_op jit(solution)/shard_map/ppermute | solution.py:277
  398.5 60.3 %collective-permute-start.27 = (bf16[4,2,128,1024]{3,2,1,0:T(8,128)(2,1)}, bf16[4,2,128,1024]{3,2,1,0:T(8,128)(2,1)}, u32[]{:S(2)}, u32[]{:S(2)}) collective-permute-start(bf16[4,2,128,1024]{3,2,1,0:T(8,128)(2,1)} %add_convert_fusion.7), channel_id=1, source_target_pairs={{0,8},{8,0},{16,24},{24,16},{1,9},{9,1},{17,25},{25,17},{2,10},{10... | collective-permute-start | bytes 6291464 | tf_op jit(solution)/shard_map/ppermute | solution.py:277
  404.1 54.6 %collective-permute-start.29 = (bf16[4,2,128,1024]{3,2,1,0:T(8,128)(2,1)}, bf16[4,2,128,1024]{3,2,1,0:T(8,128)(2,1)}, u32[]{:S(2)}, u32[]{:S(2)}) collective-permute-start(bf16[4,2,128,1024]{3,2,1,0:T(8,128)(2,1)} %add_convert_fusion.6), channel_id=1, source_target_pairs={{0,16},{8,24},{16,0},{24,8},{1,17},{9,25},{17,1},{25,9},{2,18},{10... | collective-permute-start | bytes 6291464 | tf_op jit(solution)/shard_map/ppermute | solution.py:277
  409.4 94.0 %collective-permute-start.31 = (bf16[4,2,128,1024]{3,2,1,0:T(8,128)(2,1)}, bf16[4,2,128,1024]{3,2,1,0:T(8,128)(2,1)}, u32[]{:S(2)}, u32[]{:S(2)}) collective-permute-start(bf16[4,2,128,1024]{3,2,1,0:T(8,128)(2,1)} %add_convert_fusion.5), channel_id=1, source_target_pairs={{0,24},{8,16},{16,8},{24,0},{1,25},{9,17},{17,9},{25,1},{2,26},{10... | collective-permute-start | bytes 6291464 | tf_op jit(solution)/shard_map/ppermute | solution.py:277
  527.6 129.2 %reduce-scatter.8.cloned.1.call-start = ((), (), s32[]{:S(2)}) async-start(), calls=%async_computation.13 | async-start | bytes 1769472 | tf_op jit(solution)/shard_map/reduce_scatter | solution.py:309
  528.4 51.5 %collective-permute-start.17 = (bf16[392,1024]{1,0:T(8,128)(2,1)}, bf16[392,1024]{1,0:T(8,128)(2,1)S(1)}, u32[]{:S(2)}, u32[]{:S(2)}) collective-permute-start(bf16[392,1024]{1,0:T(8,128)(2,1)} %get-tuple-element.117), channel_id=1, source_target_pairs={{0,16},{8,24},{16,0},{24,8},{1,17},{9,25},{17,1},{25,9},{2,18},{10... | collective-permute-start | bytes 2408456 | tf_op jit(solution)/shard_map/ppermute | solution.py:277
  535.5 32.1 %collective-permute-start.24 = (f32[4,128]{1,0:T(4,128)S(1)}, f32[4,128]{1,0:T(4,128)S(1)}, u32[]{:S(2)}, u32[]{:S(2)}) collective-permute-start(f32[4,128]{1,0:T(4,128)S(1)} %reduce_sum.240), channel_id=1, source_target_pairs={{0,24},{8,16},{16,8},{24,0},{1,25},{9,17},{17,9},{25,1},{2,26},{10... | collective-permute-start | bytes 6152 | tf_op jit(solution)/shard_map/ppermute | solution.py:277
  540.1 39.8 %collective-permute-start.18 = (bf16[392,1024]{1,0:T(8,128)(2,1)}, bf16[392,1024]{1,0:T(8,128)(2,1)}, u32[]{:S(2)}, u32[]{:S(2)}) collective-permute-start(bf16[392,1024]{1,0:T(8,128)(2,1)} %get-tuple-element.116), channel_id=1, source_target_pairs={{0,24},{8,16},{16,8},{24,0},{1,25},{9,17},{17,9},{25,1},{2,26},{10... | collective-permute-start | bytes 2408456 | tf_op jit(solution)/shard_map/ppermute | solution.py:277
  567.6 36.7 %collective-permute-start.20 = (bf16[392,1024]{1,0:T(8,128)(2,1)}, bf16[392,1024]{1,0:T(8,128)(2,1)}, u32[]{:S(2)}, u32[]{:S(2)}) collective-permute-start(bf16[392,1024]{1,0:T(8,128)(2,1)} %get-tuple-element.120), channel_id=1, source_target_pairs={{0,16},{8,24},{16,0},{24,8},{1,17},{9,25},{17,1},{25,9},{2,18},{10... | collective-permute-start | bytes 2408456 | tf_op jit(solution)/shard_map/ppermute | solution.py:277
  568.2 36.2 %collective-permute-start.21 = (bf16[392,1024]{1,0:T(8,128)(2,1)}, bf16[392,1024]{1,0:T(8,128)(2,1)}, u32[]{:S(2)}, u32[]{:S(2)}) collective-permute-start(bf16[392,1024]{1,0:T(8,128)(2,1)} %get-tuple-element.119), channel_id=1, source_target_pairs={{0,24},{8,16},{16,8},{24,0},{1,25},{9,17},{17,9},{25,1},{2,26},{10... | collective-permute-start | bytes 2408456 | tf_op jit(solution)/shard_map/ppermute | solution.py:277
  (93 other events, 1157.8 us)
Sparse Core Ops, SparseCore 0:
  10.2 30.1 all-gather.6
  42.5 44.7 all-gather.10
  89.0 27.8 all-gather.8
  346.4 37.3 reduce-scatter.5
  510.9 47.6 reduce-scatter.3
  610.1 33.5 reduce-scatter.7
